TPU v7x, 128 devices: a whole 4x4x4 slice. The times are simulated.
128 devices in a mesh: gx: 16 (over x_hi, z, core), gy: 8 (over x_lo, y).
Axes of the slice: x: 4 (x_hi: 2, x_lo: 2; x = x_hi * 2 + x_lo), y: 4, z: 4, core: 2. Of those that a mesh axis runs over, the one named last changes fastest.
Arguments:
- theta: float32 [32, 2048, 2048], P('gx', 'gy'), may hold values from 0.9 to 1.4
- pressure: float32 [32, 2048, 2048], P('gx', 'gy'), may hold values from 0.1 to 1
- vertical_wind: float32 [32, 2048, 2048], P('gx', 'gy'), may hold values from -6 to 6
- terrain: float32 [2048, 2048], P('gx', 'gy'), may hold values from 0 to 0.5
- column_mass: float32 [2048, 2048], P('gx', 'gy'), may hold values from 0.5 to 1
- land_mask: int32 [2048, 2048], P('gx', 'gy'), may hold values 0 or 1
- pbl_top: int32 [2048, 2048], P('gx', 'gy'), may hold values from 2 to 27
Outputs:
- updated_wind: float32 [32, 2048, 2048], P(None, 'gx', 'gy')
- geopotential: float32 [32, 2048, 2048], P(None, 'gx', 'gy')
All inputs are finite; a program needn't handle non-finite values. No bound on the sum of `land_mask` on one device may be relied on, other than what follows from the above.
Results may differ from a plain program's by a relative error of at most 0.00002.
Values sent between devices are 32-bit elements; how exact they have to be, the bound alone decides.
A program may use at most 128 MiB of HBM per device.

v0:
```python
import jax
import jax.numpy as jnp
from jax import lax
from jax.sharding import PartitionSpec as P

gamma_ratio = 1.4
smooth_rate = 0.2
lift_rate = 0.3
couple_rate = 0.5
land_boost = 0.5


def extended(x, sides, width):
    edges = {}
    for axis, dim in sides:
        count, length = (lax.axis_size(axis), x.shape[dim])
        up = [(i, (i + 1) % count) for i in range(count - 1)]
        last = lax.slice_in_dim(x, length - width, length, axis=dim)
        initial = lax.slice_in_dim(x, 0, width, axis=dim)
        edges[dim] = (
            lax.ppermute(last, axis, up),
            lax.ppermute(initial, axis, [(b, a) for a, b in up]),
        )
    done = []
    for _, dim in sides:
        low, high = edges[dim]
        around = [(width, width) if d in done else (0, 0) for d in range(x.ndim)]
        x = jnp.concatenate([jnp.pad(low, around), x, jnp.pad(high, around)], axis=dim)
        done.append(dim)
    return x


def extended_2(x, sides, width):
    for axis, dim in sides:
        count, length = (lax.axis_size(axis), x.shape[dim])
        up = [(i, (i + 1) % count) for i in range(count - 1)]
        down = [(j, i) for i, j in up]
        last = lax.slice_in_dim(x, length - width, length, axis=dim)
        initial = lax.slice_in_dim(x, 0, width, axis=dim)
        before = lax.ppermute(last, axis, up)
        after = lax.ppermute(initial, axis, down)
        x = jnp.concatenate([before, x, after], axis=dim)
    return x


def states(theta, pressure):
    alpha = theta * jnp.exp(-jnp.log(pressure) / gamma_ratio)
    sound_sq = gamma_ratio * pressure * alpha
    return (alpha, sound_sq)


def heights(terrain, column_mass, rising):
    return terrain[None] + column_mass[None] * rising / rising.shape[0]


def laplacian(padded):
    middle = padded[..., 1:-1, 1:-1]
    return (
        padded[..., 2:, 1:-1]
        + padded[..., :-2, 1:-1]
        + padded[..., 1:-1, 2:]
        + padded[..., 1:-1, :-2]
        - 4.0 * middle
    )


def column_solve(forcing, sound_sq, land_mask, pbl_top):
    levels = lax.broadcasted_iota(jnp.int32, forcing.shape, 0)
    inside = (land_mask[None] > 0) & (levels < pbl_top[None])
    damping = jnp.where(inside, 1.0 + land_boost, 1.0).astype(jnp.float32)
    couple = couple_rate * 0.5 * (sound_sq[:-1] + sound_sq[1:])
    zero_level = jnp.zeros_like(forcing[:1])
    below = jnp.concatenate([zero_level, couple], 0)
    above = jnp.concatenate([couple, zero_level], 0)
    centre = damping + below + above
    count = forcing.shape[0]
    ratios = []
    values = []
    ratio = above[0] / centre[0]
    value = forcing[0] / centre[0]
    ratios.append(ratio)
    values.append(value)
    for level in range(1, count):
        denom = centre[level] - below[level] * ratio
        value = (forcing[level] + below[level] * value) / denom
        ratio = above[level] / denom
        ratios.append(ratio)
        values.append(value)
    result = [None] * count
    current = values[count - 1]
    result[count - 1] = current
    for level in range(count - 2, -1, -1):
        current = values[level] + ratios[level] * current
        result[level] = current
    return jnp.stack(result, 0)


def on_device(theta, pressure, vertical_wind, terrain, column_mass, land_mask, pbl_top):
    theta_col, press_col, wind_col = (
        lax.all_to_all(
            lax.all_to_all(theta, "gy", split_axis=2, concat_axis=1, tiled=True),
            "gx",
            split_axis=1,
            concat_axis=0,
            tiled=True,
        ),
        lax.all_to_all(
            lax.all_to_all(pressure, "gy", split_axis=2, concat_axis=1, tiled=True),
            "gx",
            split_axis=1,
            concat_axis=0,
            tiled=True,
        ),
        lax.all_to_all(
            lax.all_to_all(vertical_wind, "gy", split_axis=2, concat_axis=1, tiled=True),
            "gx",
            split_axis=1,
            concat_axis=0,
            tiled=True,
        ),
    )
    alpha, sound_sq = states(theta_col, press_col)
    rising = jnp.cumsum(alpha, axis=0)
    wind_pad = extended(wind_col, (("gx", 1), ("gy", 2)), 1)
    geopotential = heights(terrain, column_mass, rising)
    geo_pad = extended_2(geopotential, (("gx", 1), ("gy", 2)), 1)
    forcing = wind_col + smooth_rate * laplacian(wind_pad) + lift_rate * laplacian(geo_pad)
    updated_wind = column_solve(forcing, sound_sq, land_mask, pbl_top)
    return (updated_wind, geopotential)


def solution(mesh):
    placed = (
        P("gx", "gy", None),
        P("gx", "gy", None),
        P("gx", "gy", None),
        P("gx", "gy"),
        P("gx", "gy"),
        P("gx", "gy"),
        P("gx", "gy"),
    )
    return jax.shard_map(
        on_device,
        mesh=mesh,
        in_specs=placed,
        out_specs=(P(None, "gx", "gy"), P(None, "gx", "gy")),
        check_vma=False,
    )
```

profile of v0, /device:TPU:6, one launch (start us, length us, event | category | flops | bytes accessed | tf_op | source)
XLA Modules:
  0.0 455.5 jit_solution(6270537095602682215)
XLA Ops:
  0.6 7.2 %copy.31 = f32[2,256,2048]{1,0,2:T(2,128)} copy(f32[2,256,2048]{2,1,0:T(8,128)} %param.7) | data formatting | bytes 8388608 | tf_op args[0]
  7.8 5.9 %all-to-all-start.2 = ((f32[2,256,2048]{1,0,2:T(2,128)}), f32[2,256,2048]{1,0,2:T(2,128)}, u32[]{:S(2)}, u32[]{:S(2)}) async-start(f32[2,256,2048]{1,0,2:T(2,128)} %copy.31), calls=%async_computation.2 | async-start | bytes 8388608 | tf_op jit(solution)/shard_map/all_to_all | solution.py:101
  13.8 7.2 %copy.35 = f32[2,256,2048]{1,0,2:T(2,128)} copy(f32[2,256,2048]{2,1,0:T(8,128)} %param.8) | data formatting | bytes 8388608 | tf_op args[1]
  21.0 40.8 %all-to-all-done.2 = f32[2,256,2048]{1,0,2:T(2,128)} async-done(((f32[2,256,2048]{1,0,2:T(2,128)}), f32[2,256,2048]{1,0,2:T(2,128)}, u32[]{:S(2)}, u32[]{:S(2)}) %all-to-all-start.2) | async-done | bytes 4194336 | tf_op jit(solution)/shard_map/all_to_all | solution.py:101
  61.8 5.1 %all-to-all-start.4 = ((f32[2,256,2048]{1,0,2:T(2,128)}), f32[2,256,2048]{1,0,2:T(2,128)}, u32[]{:S(2)}, u32[]{:S(2)}) async-start(f32[2,256,2048]{1,0,2:T(2,128)} %copy.35), calls=%async_computation.4 | async-start | bytes 8388608 | tf_op jit(solution)/shard_map/all_to_all | solution.py:108
  66.9 7.2 %copy.21 = f32[2,256,2048]{1,0,2:T(2,128)} copy(f32[2,256,2048]{2,1,0:T(8,128)} %param.9) | data formatting | bytes 8388608 | tf_op args[2]
  74.1 41.0 %all-to-all-done.4 = f32[2,256,2048]{1,0,2:T(2,128)} async-done(((f32[2,256,2048]{1,0,2:T(2,128)}), f32[2,256,2048]{1,0,2:T(2,128)}, u32[]{:S(2)}, u32[]{:S(2)}) %all-to-all-start.4) | async-done | bytes 4194336 | tf_op jit(solution)/shard_map/all_to_all | solution.py:108
  115.1 5.0 %all-to-all-start = ((f32[2,256,2048]{1,0,2:T(2,128)}), f32[2,256,2048]{1,0,2:T(2,128)}, u32[]{:S(2)}, u32[]{:S(2)}) async-start(f32[2,256,2048]{1,0,2:T(2,128)} %copy.21), calls=%async_computation | async-start | bytes 8388608 | tf_op jit(solution)/shard_map/all_to_all | solution.py:115
  120.1 4.5 copy.32
  124.7 5.3 %copy.33 = f32[2,8,256,256]{3,2,1,0:T(8,128)} copy(f32[2,8,256,256]{2,3,1,0:T(8,128)} %bitcast.31) | data formatting | bytes 8388608 | tf_op jit(solution)/shard_map/all_to_all | solution.py:101
  130.0 8.7 %copy.34 = f32[2,2048,256]{2,0,1:T(2,128)} copy(f32[2,2048,256]{2,1,0:T(8,128)} %bitcast.32) | data formatting | bytes 8388608 | tf_op jit(solution)/shard_map/all_to_all | solution.py:101
  138.7 29.6 %all-to-all-done = f32[2,256,2048]{1,0,2:T(2,128)} async-done(((f32[2,256,2048]{1,0,2:T(2,128)}), f32[2,256,2048]{1,0,2:T(2,128)}, u32[]{:S(2)}, u32[]{:S(2)}) %all-to-all-start) | async-done | bytes 4194336 | tf_op jit(solution)/shard_map/all_to_all | solution.py:115
  168.4 8.3 %all-to-all-start.3 = ((f32[2,2048,256]{2,0,1:T(2,128)}), f32[2,2048,256]{2,0,1:T(2,128)}, u32[]{:S(2)}, u32[]{:S(2)}) async-start(f32[2,2048,256]{2,0,1:T(2,128)} %copy.34), calls=%async_computation.3 | async-start | bytes 8388608 | tf_op jit(solution)/shard_map/all_to_all | solution.py:100
  176.7 4.5 copy.36
  181.2 5.4 %copy.37 = f32[2,8,256,256]{3,2,1,0:T(8,128)} copy(f32[2,8,256,256]{2,3,1,0:T(8,128)} %bitcast.33) | data formatting | bytes 8388608 | tf_op jit(solution)/shard_map/all_to_all | solution.py:108
  186.6 8.7 %copy.38 = f32[2,2048,256]{2,0,1:T(2,128)} copy(f32[2,2048,256]{2,1,0:T(8,128)} %bitcast.34) | data formatting | bytes 8388608 | tf_op jit(solution)/shard_map/all_to_all | solution.py:108
  195.3 35.1 %all-to-all-done.3 = f32[2,2048,256]{2,0,1:T(2,128)} async-done(((f32[2,2048,256]{2,0,1:T(2,128)}), f32[2,2048,256]{2,0,1:T(2,128)}, u32[]{:S(2)}, u32[]{:S(2)}) %all-to-all-start.3) | async-done | bytes 4194336 | tf_op jit(solution)/shard_map/all_to_all | solution.py:100
  230.4 13.0 %all-to-all-start.5 = ((f32[2,2048,256]{2,0,1:T(2,128)}), f32[2,2048,256]{2,0,1:T(2,128)}, u32[]{:S(2)}, u32[]{:S(2)}) async-start(f32[2,2048,256]{2,0,1:T(2,128)} %copy.38), calls=%async_computation.5 | async-start | bytes 8388608 | tf_op jit(solution)/shard_map/all_to_all | solution.py:107
  243.4 4.5 copy.22
  248.0 5.4 %copy.23 = f32[2,8,256,256]{3,2,1,0:T(8,128)} copy(f32[2,8,256,256]{2,3,1,0:T(8,128)} %bitcast.35) | data formatting | bytes 8388608 | tf_op jit(solution)/shard_map/all_to_all | solution.py:115
  253.4 8.7 %copy.24 = f32[2,2048,256]{2,0,1:T(2,128)} copy(f32[2,2048,256]{2,1,0:T(8,128)} %bitcast.36) | data formatting | bytes 8388608 | tf_op jit(solution)/shard_map/all_to_all | solution.py:115
  262.1 35.0 %all-to-all-done.5 = f32[2,2048,256]{2,0,1:T(2,128)} async-done(((f32[2,2048,256]{2,0,1:T(2,128)}), f32[2,2048,256]{2,0,1:T(2,128)}, u32[]{:S(2)}, u32[]{:S(2)}) %all-to-all-start.5) | async-done | bytes 4194336 | tf_op jit(solution)/shard_map/all_to_all | solution.py:107
  297.2 13.0 %all-to-all-start.1 = ((f32[2,2048,256]{2,0,1:T(2,128)}), f32[2,2048,256]{2,0,1:T(2,128)}, u32[]{:S(2)}, u32[]{:S(2)}) async-start(f32[2,2048,256]{2,0,1:T(2,128)} %copy.24), calls=%async_computation.1 | async-start | bytes 8388608 | tf_op jit(solution)/shard_map/all_to_all | solution.py:114
  310.3 4.8 %copy_multiply_fusion = (f32[2,2048,256]{2,1,0:T(8,128)S(1)}, f32[2,2048,256]{2,1,0:T(8,128)S(1)}) fusion(f32[2,2048,256]{2,0,1:T(2,128)} %all-to-all-done.3, f32[2,2048,256]{2,0,1:T(2,128)} %all-to-all-done.5), kind=kLoop, calls=%fused_computation.34 | loop fusion | flops 4194304 | bytes 16777216 | tf_op jit(solution)/shard_map/mul | solution.py:47
  319.2 7.3 %collective-permute-start.4 = (f32[32,1,256]{2,1,0:T(1,128)S(1)}, f32[32,1,256]{2,1,0:T(1,128)S(1)}, u32[]{:S(2)}, u32[]{:S(2)}) collective-permute-start(f32[32,1,256]{2,1,0:T(1,128)S(1)} %get-tuple-element.86), channel_id=1, source_target_pairs={{8,0},{16,8},{24,16},{32,24},{40,32},{48,40},{56,48},{64,56},{72,6... | collective-permute-start | bytes 98312 | tf_op jit(solution)/shard_map/ppermute | solution.py:41
  330.2 33.7 %all-to-all-done.1 = f32[2,2048,256]{2,0,1:T(2,128)} async-done(((f32[2,2048,256]{2,0,1:T(2,128)}), f32[2,2048,256]{2,0,1:T(2,128)}, u32[]{:S(2)}, u32[]{:S(2)}) %all-to-all-start.1) | async-done | bytes 4194336 | tf_op jit(solution)/shard_map/all_to_all | solution.py:114
  371.5 13.5 %collective-permute-start = (f32[32,1,256]{2,1,0:T(1,128)S(1)}, f32[32,1,256]{2,1,0:T(1,128)S(1)}, u32[]{:S(2)}, u32[]{:S(2)}) collective-permute-start(f32[32,1,256]{2,1,0:T(1,128)S(1)} %get-tuple-element.84), channel_id=1, source_target_pairs={{8,0},{16,8},{24,16},{32,24},{40,32},{48,40},{56,48},{64,56},{72,6... | collective-permute-start | bytes 98312 | tf_op jit(solution)/shard_map/ppermute | solution.py:22
  390.6 5.2 %collective-permute-start.2 = (f32[32,128,1]{1,0,2:T(8,128)S(1)}, f32[32,128,1]{1,0,2:T(8,128)S(1)}, u32[]{:S(2)}, u32[]{:S(2)}) collective-permute-start(f32[32,128,1]{1,0,2:T(8,128)S(1)} %copy.27), channel_id=1, source_target_pairs={{1,0},{2,1},{3,2},{4,3},{5,4},{6,5},{7,6},{9,8},{10,9},{11,10},{12... | collective-permute-start | bytes 49160 | tf_op jit(solution)/shard_map/ppermute | solution.py:22
  400.4 2.9 copy.42
  406.4 6.0 %collective-permute-start.6 = (f32[32,130,1]{1,0,2:T(8,128)S(1)}, f32[32,130,1]{1,0,2:T(8,128)S(1)}, u32[]{:S(2)}, u32[]{:S(2)}) collective-permute-start(f32[32,130,1]{1,0,2:T(8,128)S(1)} %copy.42), channel_id=1, source_target_pairs={{1,0},{2,1},{3,2},{4,3},{5,4},{6,5},{7,6},{9,8},{10,9},{11,10},{12... | collective-permute-start | bytes 49928 | tf_op jit(solution)/shard_map/ppermute | solution.py:41
  412.5 6.6 %pad_add_fusion = f32[32,128,256]{2,1,0:T(8,128)} fusion(f32[31,128,256]{2,1,0:T(8,128)} %fusion.15, s32[128,256]{1,0:T(8,128)S(1)} %copy-done.6, pred[128,256]{1,0:T(8,128)(4,1)S(1)} %broadcast_compare_fusion), kind=kLoop, calls=%fused_computation.35 | loop fusion | flops 5242880 | bytes 8421376 | tf_op jit(solution)/shard_map/add | solution.py:75
  426.0 24.3 %fusion.3 = f32[32,128,256]{2,1,0:T(8,128)S(1)} fusion(f32[32,130,1]{2,1,0:T(8,128)} %copy.45, f32[32,1,256]{2,1,0:T(1,128)S(1)} %collective-permute-done.4, f32[32,128,256]{2,1,0:T(8,128)} %copy-done.1, f32[32,1,256]{2,1,0:T(1,128)S(1)} %collective-permute-done.5, f32[32,130,1]{2,1,0:T(8,128)S(1)} %copy.43, f32[32,128,256]{2,1,0:T(8,128)} %bitcast.29, ...), kind=kLoop, calls=%fused_computation.5 | loop fusion | flops 37748736 | bytes 12780032 | tf_op jit(solution)/shard_map/add | solution.py:127
  (83 shorter events, 40.4 us)
Async XLA Ops:
  7.8 54.0 %all-to-all-start.2 = ((f32[2,256,2048]{1,0,2:T(2,128)}), f32[2,256,2048]{1,0,2:T(2,128)}, u32[]{:S(2)}, u32[]{:S(2)}) async-start(f32[2,256,2048]{1,0,2:T(2,128)} %copy.31), calls=%async_computation.2 | async-start | bytes 8388608 | tf_op jit(solution)/shard_map/all_to_all | solution.py:101
  61.8 53.3 %all-to-all-start.4 = ((f32[2,256,2048]{1,0,2:T(2,128)}), f32[2,256,2048]{1,0,2:T(2,128)}, u32[]{:S(2)}, u32[]{:S(2)}) async-start(f32[2,256,2048]{1,0,2:T(2,128)} %copy.35), calls=%async_computation.4 | async-start | bytes 8388608 | tf_op jit(solution)/shard_map/all_to_all | solution.py:108
  115.1 53.2 %all-to-all-start = ((f32[2,256,2048]{1,0,2:T(2,128)}), f32[2,256,2048]{1,0,2:T(2,128)}, u32[]{:S(2)}, u32[]{:S(2)}) async-start(f32[2,256,2048]{1,0,2:T(2,128)} %copy.21), calls=%async_computation | async-start | bytes 8388608 | tf_op jit(solution)/shard_map/all_to_all | solution.py:115
  168.4 62.0 %all-to-all-start.3 = ((f32[2,2048,256]{2,0,1:T(2,128)}), f32[2,2048,256]{2,0,1:T(2,128)}, u32[]{:S(2)}, u32[]{:S(2)}) async-start(f32[2,2048,256]{2,0,1:T(2,128)} %copy.34), calls=%async_computation.3 | async-start | bytes 8388608 | tf_op jit(solution)/shard_map/all_to_all | solution.py:100
  230.4 66.8 %all-to-all-start.5 = ((f32[2,2048,256]{2,0,1:T(2,128)}), f32[2,2048,256]{2,0,1:T(2,128)}, u32[]{:S(2)}, u32[]{:S(2)}) async-start(f32[2,2048,256]{2,0,1:T(2,128)} %copy.38), calls=%async_computation.5 | async-start | bytes 8388608 | tf_op jit(solution)/shard_map/all_to_all | solution.py:107
  262.1 48.1 %copy-start.7 = (s32[128,256]{1,0:T(8,128)S(1)}, s32[128,256]{1,0:T(8,128)}, u32[]{:S(2)}) copy-start(s32[128,256]{1,0:T(8,128)} %param.12) | copy-start | bytes 393220
  297.2 66.8 %all-to-all-start.1 = ((f32[2,2048,256]{2,0,1:T(2,128)}), f32[2,2048,256]{2,0,1:T(2,128)}, u32[]{:S(2)}, u32[]{:S(2)}) async-start(f32[2,2048,256]{2,0,1:T(2,128)} %copy.24), calls=%async_computation.1 | async-start | bytes 8388608 | tf_op jit(solution)/shard_map/all_to_all | solution.py:114
  315.5 0.9 copy-start.4
  315.5 1.0 copy-start.5
  317.1 10.6 %copy-start.1 = (f32[32,128,256]{2,1,0:T(8,128)}, f32[32,128,256]{2,1,0:T(8,128)S(1)}, u32[]{:S(2)}) copy-start(f32[32,128,256]{2,1,0:T(8,128)S(1)} %multiply_add_fusion) | copy-start | bytes 12582916
  317.2 73.4 %collective-permute-start.5 = (f32[32,1,256]{2,1,0:T(1,128)S(1)}, f32[32,1,256]{2,1,0:T(1,128)S(1)}, u32[]{:S(2)}, u32[]{:S(2)}) collective-permute-start(f32[32,1,256]{2,1,0:T(1,128)S(1)} %get-tuple-element.85), channel_id=1, source_target_pairs={{0,8},{8,16},{16,24},{24,32},{32,40},{40,48},{48,56},{56,64},{64,7... | collective-permute-start | bytes 98312 | tf_op jit(solution)/shard_map/ppermute | solution.py:40
  319.2 76.6 %collective-permute-start.4 = (f32[32,1,256]{2,1,0:T(1,128)S(1)}, f32[32,1,256]{2,1,0:T(1,128)S(1)}, u32[]{:S(2)}, u32[]{:S(2)}) collective-permute-start(f32[32,1,256]{2,1,0:T(1,128)S(1)} %get-tuple-element.86), channel_id=1, source_target_pairs={{8,0},{16,8},{24,16},{32,24},{40,32},{48,40},{56,48},{64,56},{72,6... | collective-permute-start | bytes 98312 | tf_op jit(solution)/shard_map/ppermute | solution.py:41
  366.9 2.6 copy-start.2
  369.6 56.4 %collective-permute-start.1 = (f32[32,1,256]{2,1,0:T(1,128)S(1)}, f32[32,1,256]{2,1,0:T(1,128)S(1)}, u32[]{:S(2)}, u32[]{:S(2)}) collective-permute-start(f32[32,1,256]{2,1,0:T(1,128)S(1)} %get-tuple-element.83), channel_id=1, source_target_pairs={{0,8},{8,16},{16,24},{24,32},{32,40},{40,48},{48,56},{56,64},{64,7... | collective-permute-start | bytes 98312 | tf_op jit(solution)/shard_map/ppermute | solution.py:21
  371.5 54.5 %collective-permute-start = (f32[32,1,256]{2,1,0:T(1,128)S(1)}, f32[32,1,256]{2,1,0:T(1,128)S(1)}, u32[]{:S(2)}, u32[]{:S(2)}) collective-permute-start(f32[32,1,256]{2,1,0:T(1,128)S(1)} %get-tuple-element.84), channel_id=1, source_target_pairs={{8,0},{16,8},{24,16},{32,24},{40,32},{48,40},{56,48},{64,56},{72,6... | collective-permute-start | bytes 98312 | tf_op jit(solution)/shard_map/ppermute | solution.py:22
  387.8 33.3 %collective-permute-start.3 = (f32[32,128,1]{1,0,2:T(8,128)S(1)}, f32[32,128,1]{1,0,2:T(8,128)S(1)}, u32[]{:S(2)}, u32[]{:S(2)}) collective-permute-start(f32[32,128,1]{1,0,2:T(8,128)S(1)} %copy.29), channel_id=1, source_target_pairs={{0,1},{1,2},{2,3},{3,4},{4,5},{5,6},{6,7},{8,9},{9,10},{10,11},{11... | collective-permute-start | bytes 49160 | tf_op jit(solution)/shard_map/ppermute | solution.py:21
  390.6 15.9 %collective-permute-start.2 = (f32[32,128,1]{1,0,2:T(8,128)S(1)}, f32[32,128,1]{1,0,2:T(8,128)S(1)}, u32[]{:S(2)}, u32[]{:S(2)}) collective-permute-start(f32[32,128,1]{1,0,2:T(8,128)S(1)} %copy.27), channel_id=1, source_target_pairs={{1,0},{2,1},{3,2},{4,3},{5,4},{6,5},{7,6},{9,8},{10,9},{11,10},{12... | collective-permute-start | bytes 49160 | tf_op jit(solution)/shard_map/ppermute | solution.py:22
  400.4 12.0 %copy-start.6 = (s32[128,256]{1,0:T(8,128)S(1)}, s32[128,256]{1,0:T(8,128)}, u32[]{:S(2)}) copy-start(s32[128,256]{1,0:T(8,128)} %param.13) | copy-start | bytes 393220
  404.5 19.3 %collective-permute-start.7 = (f32[32,130,1]{1,0,2:T(8,128)S(1)}, f32[32,130,1]{1,0,2:T(8,128)S(1)}, u32[]{:S(2)}, u32[]{:S(2)}) collective-permute-start(f32[32,130,1]{1,0,2:T(8,128)S(1)} %copy.44), channel_id=1, source_target_pairs={{0,1},{1,2},{2,3},{3,4},{4,5},{5,6},{6,7},{8,9},{9,10},{10,11},{11... | collective-permute-start | bytes 49928 | tf_op jit(solution)/shard_map/ppermute | solution.py:40
  406.4 16.6 %collective-permute-start.6 = (f32[32,130,1]{1,0,2:T(8,128)S(1)}, f32[32,130,1]{1,0,2:T(8,128)S(1)}, u32[]{:S(2)}, u32[]{:S(2)}) collective-permute-start(f32[32,130,1]{1,0,2:T(8,128)S(1)} %copy.42), channel_id=1, source_target_pairs={{1,0},{2,1},{3,2},{4,3},{5,4},{6,5},{7,6},{9,8},{10,9},{11,10},{12... | collective-permute-start | bytes 49928 | tf_op jit(solution)/shard_map/ppermute | solution.py:41
  426.0 24.3 %copy-start = (f32[31,128,256]{2,1,0:T(8,128)S(1)}, f32[31,128,256]{2,1,0:T(8,128)}, u32[]{:S(2)}) copy-start(f32[31,128,256]{2,1,0:T(8,128)} %fusion.15) | copy-start | bytes 12189700
  426.0 24.3 %copy-start.3 = (f32[32,128,256]{2,1,0:T(8,128)S(1)}, f32[32,128,256]{2,1,0:T(8,128)}, u32[]{:S(2)}) copy-start(f32[32,128,256]{2,1,0:T(8,128)} %pad_add_fusion) | copy-start | bytes 12582916
  453.5 2.0 copy-start.8
where the time goes:
time: 457 us; the launch traced here: 455 us
  waiting for transfers between devices  215 us (47%)
  local copies, waits for them, and re-layouts  103 us (23%)
  starting transfers between devices  91 us (20%)
  other arithmetic  45.4 us (10%)
    all_to_all x1, waiting for transfers between devices, on_device(): lax.all_to_all(pressure, 'gy', split_axis=2, concat_axis=1, tiled=True)  41 us
    all_to_all x1, waiting for transfers between devices, on_device(): lax.all_to_all(theta, 'gy', split_axis=2, concat_axis=1, tiled=True)  40.8 us
    all_to_all x1, waiting for transfers between devices, on_device(): lax.all_to_all(lax.all_to_all(theta, 'gy', split_axis=2, concat_axis=1, t...  35.1 us
    all_to_all x1, waiting for transfers between devices, on_device(): lax.all_to_all(lax.all_to_all(pressure, 'gy', split_axis=2, concat_axis=1...  35 us
    all_to_all x1, waiting for transfers between devices, on_device(): lax.all_to_all(lax.all_to_all(vertical_wind, 'gy', split_axis=2, concat_a...  33.7 us
    all_to_all x1, waiting for transfers between devices, on_device(): lax.all_to_all(vertical_wind, 'gy', split_axis=2, concat_axis=1, tiled=True)  29.6 us
    unnamed x36, local copies, waits for them, and re-layouts  24.4 us
    add x1, other arithmetic, on_device(): wind_col + smooth_rate * laplacian(wind_pad)  24.3 us
  transfers between devices with their start and end apart: 14, of which 6 were waited for; matrix products, arithmetic and copies ran while one was open for 24% of the time, Pallas kernels for 0%

commit v1 on v0

--- a/solution.py
+++ b/solution.py
@@ -1,6 +1,9 @@
+import functools
 import jax
 import jax.numpy as jnp
 from jax import lax
+from jax.experimental import pallas as pl
+from jax.experimental.pallas import tpu as pltpu
 from jax.sharding import PartitionSpec as P
 
 gamma_ratio = 1.4
@@ -95,30 +98,91 @@
     return jnp.stack(result, 0)
 
 
+PIECE = 32
+
+
+def send_order(steps):
+    return [
+        (a, r, shift, half, core)
+        for pair in range(2)
+        for a in range(3)
+        for r in range(steps)
+        for core in range(2)
+        for shift in (pair, pair + 2)
+        for half in range(2)
+    ]
+
+
+def relay(t_in, p_in, w_in, t_out, p_out, w_out, own, send, recv, local):
+    gx, gy = lax.axis_index("gx"), lax.axis_index("gy")
+    ins, outs = (t_in, p_in, w_in), (t_out, p_out, w_out)
+    z, c, y = (gx // 2) % 4, gx % 2, gy % 4
+    stays = (gx // 2) == gy
+
+    @pl.when(stays)
+    def _():
+        for a in range(3):
+            rows = pl.ds(pl.multiple_of(c * 128, 128), 128)
+            cols = pl.ds(pl.multiple_of(gy * 256, 256), 256)
+            pltpu.make_async_copy(ins[a].at[:, rows, cols], own.at[a], local.at[a]).start()
+
+    for a, r, shift, half, core in send_order(128 // PIECE):
+        c_to = (c + core) % 2
+        gy_to = half * 4 + (y + shift - z + 4) % 4
+        gx_to = gy * 2 + c_to
+        rows = pl.ds(pl.multiple_of(c_to * 128 + r * PIECE, PIECE), PIECE)
+        cols = pl.ds(pl.multiple_of(gy_to * 256, 256), 256)
+
+        @pl.when(jnp.logical_not((gx_to == gx) & (gy_to == gy)))
+        def _():
+            pltpu.make_async_remote_copy(
+                ins[a].at[:, rows, cols],
+                outs[a].at[pl.ds(gx * 2, 2), pl.ds(r * PIECE, PIECE)],
+                send.at[a],
+                recv.at[a],
+                device_id={"gx": gx_to, "gy": gy_to},
+                device_id_type=pl.DeviceIdType.MESH,
+            ).start()
+
+    @pl.when(stays)
+    def _():
+        for a in range(3):
+            pltpu.make_async_copy(own.at[a], own.at[a], local.at[a]).wait()
+            pltpu.make_async_copy(own.at[a], outs[a].at[pl.ds(gx * 2, 2)], local.at[a]).start()
+        for a in range(3):
+            pltpu.make_async_copy(own.at[a], own.at[a], local.at[a]).wait()
+
+    for a in range(3):
+        for count, cond in ((30, stays), (32, jnp.logical_not(stays))):
+
+            @pl.when(cond)
+            def _():
+                whole = outs[a].at[pl.ds(0, count)]
+                pltpu.make_async_copy(whole, whole, recv.at[a]).wait()
+                pltpu.make_async_copy(whole, whole, send.at[a]).wait()
+
+
+def to_tiles(theta, pressure, vertical_wind):
+    tile = jax.ShapeDtypeStruct((32, 128, 256), jnp.float32)
+    anywhere = pl.BlockSpec(memory_space=pl.ANY)
+    return pl.pallas_call(
+        relay,
+        name="relay",
+        out_shape=(tile,) * 3,
+        in_specs=[anywhere] * 3,
+        out_specs=(anywhere,) * 3,
+        scratch_shapes=[
+            pltpu.VMEM((3, 2, 128, 256), jnp.float32),
+            pltpu.SemaphoreType.DMA((3,)),
+            pltpu.SemaphoreType.DMA((3,)),
+            pltpu.SemaphoreType.DMA((3,)),
+        ],
+        compiler_params=pltpu.CompilerParams(has_side_effects=True),
+    )(theta, pressure, vertical_wind)
+
+
 def on_device(theta, pressure, vertical_wind, terrain, column_mass, land_mask, pbl_top):
-    theta_col, press_col, wind_col = (
-        lax.all_to_all(
-            lax.all_to_all(theta, "gy", split_axis=2, concat_axis=1, tiled=True),
-            "gx",
-            split_axis=1,
-            concat_axis=0,
-            tiled=True,
-        ),
-        lax.all_to_all(
-            lax.all_to_all(pressure, "gy", split_axis=2, concat_axis=1, tiled=True),
-            "gx",
-            split_axis=1,
-            concat_axis=0,
-            tiled=True,
-        ),
-        lax.all_to_all(
-            lax.all_to_all(vertical_wind, "gy", split_axis=2, concat_axis=1, tiled=True),
-            "gx",
-            split_axis=1,
-            concat_axis=0,
-            tiled=True,
-        ),
-    )
+    theta_col, press_col, wind_col = to_tiles(theta, pressure, vertical_wind)
     alpha, sound_sq = states(theta_col, press_col)
     rising = jnp.cumsum(alpha, axis=0)
     wind_pad = extended(wind_col, (("gx", 1), ("gy", 2)), 1)

time: 457 us -> 255 us (0.56)
  waiting for transfers between devices: 215 us -> 0.02 us
  Pallas kernels: 0 us -> 150 us
  local copies, waits for them, and re-layouts: 103 us -> 21.3 us
  starting transfers between devices: 91 us -> 34.4 us
    all_to_all x6 -> x0, waiting for transfers between devices: 215 us -> none  [the longest x1 41 us: on_device(): lax.all_to_all(pressure, 'gy', split_axis=2, concat_axis=1, tiled=True)]
    pallas_call x0 -> x1, Pallas kernels: none -> 150 us  [to_tiles(): pl.pallas_call(relay, name='relay', out_shape=(tile,) * 3, in_specs=[anyw...]
    all_to_all x11 -> x0, local copies, waits for them, and re-layouts: 58.9 us -> none  [the longest x3 18.7 us: on_device(): lax.all_to_all(vertical_wind, 'gy', split_axis=2, concat_axis=1, tiled=True)]
    all_to_all x6 -> x0, starting transfers between devices: 50.4 us -> none  [the longest x1 13 us: on_device(): lax.all_to_all(lax.all_to_all(pressure, 'gy', split_axis=2, concat_axis=1...]
    unnamed x36 -> x33, local copies, waits for them, and re-layouts: 24.4 us -> 2.22 us
    ppermute x2, starting transfers between devices: 18.7 us -> 10.5 us  [extended(): lax.ppermute(initial, axis, [(b, a) for a, b in up])]
    mul x1 -> x0, other arithmetic: 4.82 us -> none  [states(): alpha = theta * jnp.exp(-jnp.log(pressure) / gamma_ratio)]
  transfers between devices with their start and end apart: 14 -> 8, of which waited for: 6 -> 0; matrix products, arithmetic and copies ran while one was open for 24% -> 15% of each run, Pallas kernels for 0% -> 0%
where the time goes in v1:
time: 255 us; the launch traced here: 254 us
  Pallas kernels  150 us (59%)
  other arithmetic  47.9 us (19%)
  starting transfers between devices  34.4 us (13%)
  local copies, waits for them, and re-layouts  21.3 us (8%)
    pallas_call x1, Pallas kernels, to_tiles(): pl.pallas_call(relay, name='relay', out_shape=(tile,) * 3, in_specs=[anyw...  150 us
    add x1, other arithmetic, on_device(): wind_col + smooth_rate * laplacian(wind_pad)  24.3 us
    ppermute x2, starting transfers between devices, extended_2(): after = lax.ppermute(initial, axis, down)  13.2 us
    ppermute x2, starting transfers between devices, extended(): lax.ppermute(initial, axis, [(b, a) for a, b in up])  10.5 us
    ppermute x2, starting transfers between devices, extended(): lax.ppermute(last, axis, up)  6.64 us
    add x1, other arithmetic, column_solve(): centre = damping + below + above  6.63 us
  transfers between devices with their start and end apart: 8, of which 0 were waited for; matrix products, arithmetic and copies ran while one was open for 15% of the time, Pallas kernels for 0%

profile of v1, /device:TPU:6, one launch (start us, length us, event | category | flops | bytes accessed | tf_op | source)
XLA Modules:
  0.0 254.3 jit_solution(1141418246407945593)
XLA Ops:
  0.7 149.6 %relay.1 = (f32[32,128,256]{2,1,0:T(8,128)}, f32[32,128,256]{2,1,0:T(8,128)}, f32[32,128,256]{2,1,0:T(8,128)}) custom-call(f32[2,256,2048]{2,1,0:T(8,128)} %t_in.1, f32[2,256,2048]{2,1,0:T(8,128)} %p_in.1, f32[2,256,2048]{2,1,0:T(8,128)} %w_in.1), custom_call_target="tpu_custom_call" | custom-call | tf_op jit(solution)/shard_map/relay/pallas_call | solution.py:168
  150.2 1.1 fusion.82
  151.3 2.3 collective-permute-start.1
  153.6 6.9 %collective-permute-start = (f32[32,1,256]{2,1,0:T(1,128)S(1)}, f32[32,1,256]{2,1,0:T(1,128)S(1)}, u32[]{:S(2)}, u32[]{:S(2)}) collective-permute-start(f32[32,1,256]{2,1,0:T(1,128)S(1)} %get-tuple-element.90), channel_id=1, source_target_pairs={{8,0},{16,8},{24,16},{32,24},{40,32},{48,40},{56,48},{64,56},{72,6... | collective-permute-start | bytes 98312 | tf_op jit(solution)/shard_map/ppermute | solution.py:25
  160.5 4.4 %multiply_add_fusion = f32[32,128,256]{2,1,0:T(8,128)S(1)} fusion(f32[32,128,256]{2,1,0:T(8,128)} %get-tuple-element.6, f32[32,128,256]{2,1,0:T(8,128)} %get-tuple-element.7, f32[128,256]{1,0:T(8,128)S(1)} %copy-done.4, f32[128,256]{1,0:T(8,128)S(1)} %copy-done.5), kind=kOutput, calls=%fused_computation.36 | output fusion | flops 38797312 | bytes 12845056 | tf_op jit(solution)/shard_map/jit(cumsum)/reduce_window_sum | solution.py:187
  165.0 0.0 copy-start.1
  165.0 1.9 collective-permute-start.5
  167.0 7.3 %collective-permute-start.4 = (f32[32,1,256]{2,1,0:T(1,128)S(1)}, f32[32,1,256]{2,1,0:T(1,128)S(1)}, u32[]{:S(2)}, u32[]{:S(2)}) collective-permute-start(f32[32,1,256]{2,1,0:T(1,128)S(1)} %get-tuple-element.92), channel_id=1, source_target_pairs={{8,0},{16,8},{24,16},{32,24},{40,32},{48,40},{56,48},{64,56},{72,6... | collective-permute-start | bytes 98312 | tf_op jit(solution)/shard_map/ppermute | solution.py:44
  174.2 2.1 fusion.81
  176.3 2.2 copy.11
  178.5 4.3 %collective-permute-start.3 = (f32[32,128,1]{1,0,2:T(8,128)S(1)}, f32[32,128,1]{1,0,2:T(8,128)S(1)}, u32[]{:S(2)}, u32[]{:S(2)}) collective-permute-start(f32[32,128,1]{1,0,2:T(8,128)S(1)} %copy.11), channel_id=1, source_target_pairs={{0,1},{1,2},{2,3},{3,4},{4,5},{5,6},{6,7},{8,9},{9,10},{10,11},{11... | collective-permute-start | bytes 49160 | tf_op jit(solution)/shard_map/ppermute | solution.py:24
  182.9 4.7 %multiply_multiply_fusion = f32[32,128,256]{2,1,0:T(8,128)S(1)} fusion(f32[32,128,256]{2,1,0:T(8,128)} %get-tuple-element.7, f32[32,128,256]{2,1,0:T(8,128)} %get-tuple-element.6), kind=kLoop, calls=%fused_computation.34 | loop fusion | flops 5242880 | bytes 12582912 | tf_op jit(solution)/shard_map/mul | solution.py:51
  187.6 0.0 copy-start.7
  187.6 2.5 fusion.15
  190.1 0.6 copy.9
  190.8 3.6 %collective-permute-start.2 = (f32[32,128,1]{1,0,2:T(8,128)S(1)}, f32[32,128,1]{1,0,2:T(8,128)S(1)}, u32[]{:S(2)}, u32[]{:S(2)}) collective-permute-start(f32[32,128,1]{1,0,2:T(8,128)S(1)} %copy.9), channel_id=1, source_target_pairs={{1,0},{2,1},{3,2},{4,3},{5,4},{6,5},{7,6},{9,8},{10,9},{11,10},{12... | collective-permute-start | bytes 49160 | tf_op jit(solution)/shard_map/ppermute | solution.py:25
  194.4 2.6 %pad_maximum_fusion = f32[32,130,256]{2,1,0:T(8,128)S(1)} fusion(f32[32,1,256]{2,1,0:T(1,128)S(1)} %collective-permute-done.4, f32[32,128,256]{2,1,0:T(8,128)} %copy-done.1, f32[32,1,256]{2,1,0:T(1,128)S(1)} %collective-permute-done.5), kind=kLoop, calls=%fused_computation | loop fusion | flops 2129920 | bytes 8519680 | tf_op jit(solution)/shard_map/concatenate | solution.py:45
  197.0 2.1 fusion.80
  199.0 2.9 %copy.13 = f32[32,130,1]{1,0,2:T(8,128)S(1)} copy(f32[32,130,1]{2,1,0:T(8,128)} %get-tuple-element.85) | data formatting | bytes 33280 | tf_op jit(solution)/shard_map/slice | solution.py:42
  201.9 1.2 copy.15
  203.1 2.2 collective-permute-start.7
  205.4 5.9 %collective-permute-start.6 = (f32[32,130,1]{1,0,2:T(8,128)S(1)}, f32[32,130,1]{1,0,2:T(8,128)S(1)}, u32[]{:S(2)}, u32[]{:S(2)}) collective-permute-start(f32[32,130,1]{1,0,2:T(8,128)S(1)} %copy.13), channel_id=1, source_target_pairs={{1,0},{2,1},{3,2},{4,3},{5,4},{6,5},{7,6},{9,8},{10,9},{11,10},{12... | collective-permute-start | bytes 49928 | tf_op jit(solution)/shard_map/ppermute | solution.py:44
  211.3 6.6 %pad_add_fusion = f32[32,128,256]{2,1,0:T(8,128)} fusion(f32[31,128,256]{2,1,0:T(8,128)} %fusion.15, s32[128,256]{1,0:T(8,128)S(1)} %copy-done.6, pred[128,256]{1,0:T(8,128)(4,1)S(1)} %broadcast_compare_fusion), kind=kLoop, calls=%fused_computation.33 | loop fusion | flops 5242880 | bytes 8421376 | tf_op jit(solution)/shard_map/add | solution.py:78
  217.9 2.0 copy.10
  219.9 2.0 copy.12
  221.9 0.7 copy.14
  222.6 2.2 copy.16
  224.8 24.3 %fusion.3 = f32[32,128,256]{2,1,0:T(8,128)S(1)} fusion(f32[32,130,1]{2,1,0:T(8,128)} %copy.16, f32[32,1,256]{2,1,0:T(1,128)S(1)} %collective-permute-done.4, f32[32,128,256]{2,1,0:T(8,128)} %copy-done.1, f32[32,1,256]{2,1,0:T(1,128)S(1)} %collective-permute-done.5, f32[32,130,1]{2,1,0:T(8,128)S(1)} %copy.14, f32[32,128,256]{2,1,0:T(8,128)} %get-tuple-element.5, ...), kind=kLoop, calls=%fused_computation.5 | loop fusion | flops 37748736 | bytes 12780032 | tf_op jit(solution)/shard_map/add | solution.py:191
  249.1 1.5 fusion.20
  250.7 0.8 add_dynamic-update-slice_fusion
  252.3 0.0 copy-start.8
  252.3 2.0 copy-done.8
  (55 shorter events, 0.7 us)
Async XLA Ops:
  0.6 159.9 %copy-start.4 = (f32[128,256]{1,0:T(8,128)S(1)}, f32[128,256]{1,0:T(8,128)}, u32[]{:S(2)}) copy-start(f32[128,256]{1,0:T(8,128)} %param.11) | copy-start | bytes 393220
  0.6 159.9 %copy-start.5 = (f32[128,256]{1,0:T(8,128)S(1)}, f32[128,256]{1,0:T(8,128)}, u32[]{:S(2)}) copy-start(f32[128,256]{1,0:T(8,128)} %param.10) | copy-start | bytes 393220
  151.3 73.5 %collective-permute-start.1 = (f32[32,1,256]{2,1,0:T(1,128)S(1)}, f32[32,1,256]{2,1,0:T(1,128)S(1)}, u32[]{:S(2)}, u32[]{:S(2)}) collective-permute-start(f32[32,1,256]{2,1,0:T(1,128)S(1)} %get-tuple-element.89), channel_id=1, source_target_pairs={{0,8},{8,16},{16,24},{24,32},{32,40},{40,48},{48,56},{56,64},{64,7... | collective-permute-start | bytes 98312 | tf_op jit(solution)/shard_map/ppermute | solution.py:24
  153.6 71.2 %collective-permute-start = (f32[32,1,256]{2,1,0:T(1,128)S(1)}, f32[32,1,256]{2,1,0:T(1,128)S(1)}, u32[]{:S(2)}, u32[]{:S(2)}) collective-permute-start(f32[32,1,256]{2,1,0:T(1,128)S(1)} %get-tuple-element.90), channel_id=1, source_target_pairs={{8,0},{16,8},{24,16},{32,24},{40,32},{48,40},{56,48},{64,56},{72,6... | collective-permute-start | bytes 98312 | tf_op jit(solution)/shard_map/ppermute | solution.py:25
  160.5 13.7 %copy-start.3 = (f32[32,128,256]{2,1,0:T(8,128)S(1)}, f32[32,128,256]{2,1,0:T(8,128)}, u32[]{:S(2)}) copy-start(f32[32,128,256]{2,1,0:T(8,128)} %get-tuple-element.5) | copy-start | bytes 12582916
  165.0 11.4 %copy-start.1 = (f32[32,128,256]{2,1,0:T(8,128)}, f32[32,128,256]{2,1,0:T(8,128)S(1)}, u32[]{:S(2)}) copy-start(f32[32,128,256]{2,1,0:T(8,128)S(1)} %multiply_add_fusion) | copy-start | bytes 12582916
  165.0 25.7 %collective-permute-start.5 = (f32[32,1,256]{2,1,0:T(1,128)S(1)}, f32[32,1,256]{2,1,0:T(1,128)S(1)}, u32[]{:S(2)}, u32[]{:S(2)}) collective-permute-start(f32[32,1,256]{2,1,0:T(1,128)S(1)} %get-tuple-element.91), channel_id=1, source_target_pairs={{0,8},{8,16},{16,24},{24,32},{32,40},{40,48},{48,56},{56,64},{64,7... | collective-permute-start | bytes 98312 | tf_op jit(solution)/shard_map/ppermute | solution.py:43
  167.0 27.4 %collective-permute-start.4 = (f32[32,1,256]{2,1,0:T(1,128)S(1)}, f32[32,1,256]{2,1,0:T(1,128)S(1)}, u32[]{:S(2)}, u32[]{:S(2)}) collective-permute-start(f32[32,1,256]{2,1,0:T(1,128)S(1)} %get-tuple-element.92), channel_id=1, source_target_pairs={{8,0},{16,8},{24,16},{32,24},{40,32},{48,40},{56,48},{64,56},{72,6... | collective-permute-start | bytes 98312 | tf_op jit(solution)/shard_map/ppermute | solution.py:44
  178.5 41.4 %collective-permute-start.3 = (f32[32,128,1]{1,0,2:T(8,128)S(1)}, f32[32,128,1]{1,0,2:T(8,128)S(1)}, u32[]{:S(2)}, u32[]{:S(2)}) collective-permute-start(f32[32,128,1]{1,0,2:T(8,128)S(1)} %copy.11), channel_id=1, source_target_pairs={{0,1},{1,2},{2,3},{3,4},{4,5},{5,6},{6,7},{8,9},{9,10},{10,11},{11... | collective-permute-start | bytes 49160 | tf_op jit(solution)/shard_map/ppermute | solution.py:24
  187.6 2.5 copy-start.7
  190.8 14.6 %collective-permute-start.2 = (f32[32,128,1]{1,0,2:T(8,128)S(1)}, f32[32,128,1]{1,0,2:T(8,128)S(1)}, u32[]{:S(2)}, u32[]{:S(2)}) collective-permute-start(f32[32,128,1]{1,0,2:T(8,128)S(1)} %copy.9), channel_id=1, source_target_pairs={{1,0},{2,1},{3,2},{4,3},{5,4},{6,5},{7,6},{9,8},{10,9},{11,10},{12... | collective-permute-start | bytes 49160 | tf_op jit(solution)/shard_map/ppermute | solution.py:25
  199.0 12.2 %copy-start.6 = (s32[128,256]{1,0:T(8,128)S(1)}, s32[128,256]{1,0:T(8,128)}, u32[]{:S(2)}) copy-start(s32[128,256]{1,0:T(8,128)} %param.13) | copy-start | bytes 393220
  203.1 19.5 %collective-permute-start.7 = (f32[32,130,1]{1,0,2:T(8,128)S(1)}, f32[32,130,1]{1,0,2:T(8,128)S(1)}, u32[]{:S(2)}, u32[]{:S(2)}) collective-permute-start(f32[32,130,1]{1,0,2:T(8,128)S(1)} %copy.15), channel_id=1, source_target_pairs={{0,1},{1,2},{2,3},{3,4},{4,5},{5,6},{6,7},{8,9},{9,10},{10,11},{11... | collective-permute-start | bytes 49928 | tf_op jit(solution)/shard_map/ppermute | solution.py:43
  205.4 16.5 %collective-permute-start.6 = (f32[32,130,1]{1,0,2:T(8,128)S(1)}, f32[32,130,1]{1,0,2:T(8,128)S(1)}, u32[]{:S(2)}, u32[]{:S(2)}) collective-permute-start(f32[32,130,1]{1,0,2:T(8,128)S(1)} %copy.13), channel_id=1, source_target_pairs={{1,0},{2,1},{3,2},{4,3},{5,4},{6,5},{7,6},{9,8},{10,9},{11,10},{12... | collective-permute-start | bytes 49928 | tf_op jit(solution)/shard_map/ppermute | solution.py:44
  224.8 24.3 %copy-start = (f32[31,128,256]{2,1,0:T(8,128)S(1)}, f32[31,128,256]{2,1,0:T(8,128)}, u32[]{:S(2)}) copy-start(f32[31,128,256]{2,1,0:T(8,128)} %fusion.15) | copy-start | bytes 12189700
  224.8 24.3 %copy-start.2 = (f32[32,128,256]{2,1,0:T(8,128)S(1)}, f32[32,128,256]{2,1,0:T(8,128)}, u32[]{:S(2)}) copy-start(f32[32,128,256]{2,1,0:T(8,128)} %pad_add_fusion) | copy-start | bytes 12582916
  252.3 2.0 copy-start.8

commit v2 on v0

v2 whole, which is shorter than its diff:
```python
import jax
import jax.numpy as jnp
from jax import lax
from jax.experimental import pallas as pl
from jax.experimental.pallas import tpu as pltpu
from jax.sharding import PartitionSpec as P

gamma_ratio = 1.4
smooth_rate = 0.2
lift_rate = 0.3
couple_rate = 0.5
land_boost = 0.5

LEVELS, ROWS, COLS = 32, 128, 256
SLAB_ROWS, SLAB_COLS = 256, 2048
PIECE = 32
BAND = 16
MIB = 1024 * 1024


def remote(src, dst, send, recv, gx, gy):
    return pltpu.make_async_remote_copy(
        src, dst, send, recv, device_id={"gx": gx, "gy": gy}, device_id_type=pl.DeviceIdType.MESH
    )


def await_bytes(ref, sem):
    pltpu.make_async_copy(ref, ref, sem).wait()


def send_pieces(srcs, dsts, sends, recvs, pair):
    gx, gy = lax.axis_index("gx"), lax.axis_index("gy")
    z, c, y = (gx // 2) % 4, gx % 2, gy % 4
    starts = []
    for a in range(len(srcs)):
        for r in range(ROWS // PIECE):
            for core in range(2):
                for shift in (pair, pair + 2):
                    for half in range(2):
                        starts.append((a, r, core, shift, half))
    for a, r, core, shift, half in starts:
        c_to = (c + core) % 2
        gx_to = gy * 2 + c_to
        gy_to = half * 4 + (y + shift - z + 4) % 4
        rows = pl.ds(pl.multiple_of(c_to * ROWS + r * PIECE, PIECE), PIECE)
        cols = pl.ds(pl.multiple_of(gy_to * COLS, COLS), COLS)

        @pl.when(jnp.logical_not((gx_to == gx) & (gy_to == gy)))
        def _():
            remote(
                srcs[a].at[:, rows, cols],
                dsts[a].at[pl.ds(gx * 2, 2), pl.ds(r * PIECE, PIECE)],
                sends[a],
                recvs[a],
                gx_to,
                gy_to,
            ).start()


def smooth_wind(wind, smoothed):
    sub = lax.broadcasted_iota(jnp.int32, (8, SLAB_COLS), 0)
    lane = lax.broadcasted_iota(jnp.int32, (8, SLAB_COLS), 1)
    for level in range(2):

        def block(b, _):
            at = pl.multiple_of(b * 8, 8)
            before = wind[level, pl.ds(at, 8), :]
            here = wind[level, pl.ds(pl.multiple_of(at + 8, 8), 8), :]
            after = wind[level, pl.ds(pl.multiple_of(at + 16, 8), 8), :]
            low = jnp.where(sub == 0, pltpu.roll(before, 1, 0), pltpu.roll(here, 1, 0))
            high = jnp.where(sub == 7, pltpu.roll(after, 7, 0), pltpu.roll(here, 7, 0))
            left = jnp.where(lane == 0, 0.0, pltpu.roll(here, 1, 1))
            right = jnp.where(lane == SLAB_COLS - 1, 0.0, pltpu.roll(here, SLAB_COLS - 1, 1))
            lap = high + low + right + left - 4.0 * here
            smoothed[level, pl.ds(at, 8), :] = here + smooth_rate * lap
            return 0

        lax.fori_loop(0, SLAB_ROWS // 8, block, 0)


def columns(theta, press, terrain, mass, land, top, geo, couple, inverse):
    def band(b, _):
        rows = pl.ds(pl.multiple_of(b * BAND, BAND), BAND)
        ground, weight = terrain[rows, :], mass[rows, :]
        limit = jnp.where(land[rows, :] > 0, top[rows, :], 0)

        def state(k, rising):
            p = press[k, rows, :]
            alpha = theta[k, rows, :] * jnp.exp(-jnp.log(p) / gamma_ratio)
            rising = rising + alpha
            geo[k, rows, :] = ground + weight * rising / LEVELS
            return rising, gamma_ratio * p * alpha

        def eliminate(k, below, above, ratio):
            damping = jnp.where(k < limit, 1.0 + land_boost, 1.0)
            denom = damping + below + above - below * ratio
            inv = 1.0 / denom
            inverse[k, rows, :] = inv
            couple[k, rows, :] = above
            return above * inv

        def level(k, carry):
            rising, sound_low, below, ratio = carry
            rising, sound = state(k, rising)
            above = couple_rate * 0.5 * (sound_low + sound)
            ratio = eliminate(k - 1, below, above, ratio)
            return rising, sound, above, ratio

        zero = jnp.zeros((BAND, COLS), jnp.float32)
        rising, sound = state(0, zero)
        _, _, below, ratio = lax.fori_loop(1, LEVELS, level, (rising, sound, zero, zero))
        eliminate(LEVELS - 1, below, zero, ratio)
        return 0

    lax.fori_loop(0, ROWS // BAND, band, 0)


def pack_columns(geo, packed):
    lane = lax.broadcasted_iota(jnp.int32, (ROWS, 128), 1)
    packed[...] = jnp.zeros_like(packed)

    def level(k, _):
        last = pltpu.roll(geo[k, :, COLS - 128 :], k + 1, 1)
        first = pltpu.roll(geo[k, :, :128], k, 1)
        packed[0] = jnp.where(lane == k, last, packed[0])
        packed[1] = jnp.where(lane == k, first, packed[1])
        return 0

    lax.fori_loop(0, LEVELS, level, 0)


def lift(geo, edge_rows, edge_cols, out):
    sub = lax.broadcasted_iota(jnp.int32, (ROWS, COLS), 0)
    lane = lax.broadcasted_iota(jnp.int32, (ROWS, 128), 1)

    def level(k, _):
        here = geo[k]
        low = jnp.where(sub == 0, edge_rows[0, k], pltpu.roll(here, 1, 0))
        high = jnp.where(sub == ROWS - 1, edge_rows[1, k], pltpu.roll(here, ROWS - 1, 0))
        left = pltpu.roll(here, 1, 1)
        right = pltpu.roll(here, COLS - 1, 1)
        from_left = pltpu.roll(edge_cols[0], 128 - k, 1)
        from_right = pltpu.roll(edge_cols[1], 127 - k, 1)
        for half in range(2):
            part = slice(half * 128, half * 128 + 128)
            l, r = left[:, part], right[:, part]
            if half == 0:
                l = jnp.where(lane == 0, from_left, l)
            else:
                r = jnp.where(lane == 127, from_right, r)
            lap = high[:, part] + low[:, part] + r + l - 4.0 * here[:, part]
            out[k, :, part] = lift_rate * lap
        return 0

    lax.fori_loop(0, LEVELS, level, 0)


def gather(
    theta_in, press_in, wind_in, terrain_in, mass_in, land_in, top_in,
    forcing, lifted, couple, inverse, geo,
    theta, press, wind, smoothed, terrain, mass, land, top,
    edge_rows, edge_cols, packed, send, recv, edge_send, edge_recv, local,
):
    gx, gy = lax.axis_index("gx"), lax.axis_index("gy")
    c = gx % 2
    stays = (gx // 2) == gy
    own_rows = pl.ds(pl.multiple_of(c * ROWS, ROWS), ROWS)
    own_cols = pl.ds(pl.multiple_of(gy * COLS, COLS), COLS)
    own_levels = pl.ds(gx * 2, 2)
    inner = pl.ds(8, SLAB_ROWS)

    wind_up = remote(
        wind_in.at[:, pl.ds(SLAB_ROWS - 1, 1), :], wind.at[:, pl.ds(7, 1), :],
        edge_send.at[0], edge_recv.at[0], gx, (gy + 1) % 8,
    )
    wind_down = remote(
        wind_in.at[:, pl.ds(0, 1), :], wind.at[:, pl.ds(8 + SLAB_ROWS, 1), :],
        edge_send.at[1], edge_recv.at[1], gx, (gy + 7) % 8,
    )
    geo_up = remote(
        geo.at[:, pl.ds(ROWS - 1, 1), :], edge_rows.at[0],
        edge_send.at[2], edge_recv.at[2], (gx + 1) % 16, gy,
    )
    geo_down = remote(
        geo.at[:, pl.ds(0, 1), :], edge_rows.at[1],
        edge_send.at[3], edge_recv.at[3], (gx + 15) % 16, gy,
    )
    geo_right = remote(
        packed.at[0], edge_cols.at[0], edge_send.at[4], edge_recv.at[4], gx, (gy + 1) % 8
    )
    geo_left = remote(
        packed.at[1], edge_cols.at[1], edge_send.at[5], edge_recv.at[5], gx, (gy + 7) % 8
    )
    low_x, high_x, low_y, high_y = gx > 0, gx < 15, gy > 0, gy < 7

    pl.when(high_y)(lambda: wind_up.start())
    pl.when(low_y)(lambda: wind_down.start())
    loads = [
        pltpu.make_async_copy(wind_in, wind.at[:, inner, :], local.at[0]),
        pltpu.make_async_copy(terrain_in, terrain, local.at[1]),
        pltpu.make_async_copy(mass_in, mass, local.at[2]),
        pltpu.make_async_copy(land_in, land, local.at[3]),
        pltpu.make_async_copy(top_in, top, local.at[4]),
    ]
    own = [
        pltpu.make_async_copy(
            src.at[:, own_rows, own_cols], dst.at[own_levels], local.at[5 + a]
        )
        for a, (src, dst) in enumerate(((theta_in, theta), (press_in, press)))
    ]
    for pair in range(2):
        send_pieces(
            (theta_in, press_in), (theta, press),
            (send.at[0], send.at[1]), (recv.at[0], recv.at[1]), pair,
        )
    for load in loads:
        load.start()

    @pl.when(stays)
    def _():
        for copy in own:
            copy.start()

    blank = jnp.zeros((1, SLAB_COLS), jnp.float32)

    @pl.when(jnp.logical_not(low_y))
    def _():
        for level in range(2):
            wind[level, pl.ds(7, 1), :] = blank

    @pl.when(jnp.logical_not(high_y))
    def _():
        for level in range(2):
            wind[level, pl.ds(8 + SLAB_ROWS, 1), :] = blank

    loads[0].wait()
    pl.when(low_y)(lambda: wind_up.wait_recv())
    pl.when(high_y)(lambda: wind_down.wait_recv())
    smooth_wind(wind, smoothed)

    @pl.when(stays)
    def _():
        for level in range(2):
            forcing[gx * 2 + level] = smoothed[level, own_rows, own_cols]

    send_pieces((smoothed,), (forcing,), (send.at[2],), (recv.at[2],), 0)

    for load in loads[1:]:
        load.wait()

    @pl.when(stays)
    def _():
        for a, dst in enumerate((theta, press)):
            own[a].wait()
            await_bytes(dst.at[pl.ds(0, LEVELS - 2)], recv.at[a])

    @pl.when(jnp.logical_not(stays))
    def _():
        for a, dst in enumerate((theta, press)):
            await_bytes(dst, recv.at[a])

    columns(theta, press, terrain, mass, land, top, geo, couple, inverse)
    pack_columns(geo, packed)

    @pl.when(jnp.logical_not(low_x))
    def _():
        edge_rows[0] = jnp.zeros((LEVELS, 1, COLS), jnp.float32)

    @pl.when(jnp.logical_not(high_x))
    def _():
        edge_rows[1] = jnp.zeros((LEVELS, 1, COLS), jnp.float32)

    @pl.when(jnp.logical_not(low_y))
    def _():
        edge_cols[0] = jnp.zeros((ROWS, 128), jnp.float32)

    @pl.when(jnp.logical_not(high_y))
    def _():
        edge_cols[1] = jnp.zeros((ROWS, 128), jnp.float32)

    pl.when(high_x)(lambda: geo_up.start())
    pl.when(low_x)(lambda: geo_down.start())
    pl.when(high_y)(lambda: geo_right.start())
    pl.when(low_y)(lambda: geo_left.start())
    send_pieces((smoothed,), (forcing,), (send.at[2],), (recv.at[2],), 1)

    pl.when(low_x)(lambda: geo_up.wait_recv())
    pl.when(high_x)(lambda: geo_down.wait_recv())
    pl.when(low_y)(lambda: geo_right.wait_recv())
    pl.when(high_y)(lambda: geo_left.wait_recv())
    lift(geo, edge_rows, edge_cols, lifted)

    for cond, copies in (
        (high_x, (geo_up,)),
        (low_x, (geo_down,)),
        (high_y, (wind_up, geo_right)),
        (low_y, (wind_down, geo_left)),
    ):

        @pl.when(cond)
        def _():
            for copy in copies:
                copy.wait_send()

    for count, cond in ((LEVELS - 2, stays), (LEVELS, jnp.logical_not(stays))):

        @pl.when(cond)
        def _():
            await_bytes(forcing.at[pl.ds(0, count)], recv.at[2])
            for a, ref in enumerate((theta, press, forcing)):
                await_bytes(ref.at[pl.ds(0, count)], send.at[a])


def finish(forcing, lifted, couple, inverse, geo_in, wind, geo_out, sem):
    step, steps = pl.program_id(0), pl.num_programs(0)
    rows = pl.ds(pl.multiple_of(step * BAND, BAND), BAND)
    copy = pltpu.make_async_copy(geo_in, geo_out, sem)
    pl.when(step == 0)(lambda: copy.start())
    value = (forcing[0, rows, :] + lifted[0, rows, :]) * inverse[0, rows, :]
    wind[0] = value
    for k in range(1, LEVELS):
        below = couple[k - 1, rows, :]
        value = (forcing[k, rows, :] + lifted[k, rows, :] + below * value) * inverse[k, rows, :]
        wind[k] = value
    for k in range(LEVELS - 2, -1, -1):
        value = wind[k] + couple[k, rows, :] * inverse[k, rows, :] * value
        wind[k] = value
    pl.when(step == steps - 1)(lambda: copy.wait())


def on_device(*args):
    tile = jax.ShapeDtypeStruct((LEVELS, ROWS, COLS), jnp.float32)
    hbm = pl.BlockSpec(memory_space=pltpu.HBM)
    vmem = pl.BlockSpec(memory_space=pltpu.VMEM)
    f32, i32 = jnp.float32, jnp.int32
    parts = pl.pallas_call(
        gather,
        name="gather",
        out_shape=(tile,) * 5,
        in_specs=[hbm] * 7,
        out_specs=(vmem,) * 5,
        scratch_shapes=[
            pltpu.VMEM((LEVELS, ROWS, COLS), f32),
            pltpu.VMEM((LEVELS, ROWS, COLS), f32),
            pltpu.VMEM((2, SLAB_ROWS + 16, SLAB_COLS), f32),
            pltpu.VMEM((2, SLAB_ROWS, SLAB_COLS), f32),
            pltpu.VMEM((ROWS, COLS), f32),
            pltpu.VMEM((ROWS, COLS), f32),
            pltpu.VMEM((ROWS, COLS), i32),
            pltpu.VMEM((ROWS, COLS), i32),
            pltpu.VMEM((2, LEVELS, 1, COLS), f32),
            pltpu.VMEM((2, ROWS, 128), f32),
            pltpu.VMEM((2, ROWS, 128), f32),
            pltpu.SemaphoreType.DMA((3,)),
            pltpu.SemaphoreType.DMA((3,)),
            pltpu.SemaphoreType.DMA((6,)),
            pltpu.SemaphoreType.DMA((6,)),
            pltpu.SemaphoreType.DMA((7,)),
        ],
        compiler_params=pltpu.CompilerParams(has_side_effects=True, vmem_limit_bytes=30 * MIB),
    )(*args)
    return pl.pallas_call(
        finish,
        name="finish",
        grid=(ROWS // BAND,),
        out_shape=(tile, tile),
        in_specs=[vmem] * 5,
        out_specs=(pl.BlockSpec((LEVELS, BAND, COLS), lambda i: (0, i, 0)), hbm),
        scratch_shapes=[pltpu.SemaphoreType.DMA],
        compiler_params=pltpu.CompilerParams(vmem_limit_bytes=8 * MIB),
    )(*parts)


def solution(mesh):
    slab, tile = P("gx", "gy", None), P("gx", "gy")
    return jax.shard_map(
        on_device,
        mesh=mesh,
        in_specs=(slab,) * 3 + (tile,) * 4,
        out_specs=(P(None, "gx", "gy"),) * 2,
        check_vma=False,
    )
```

time: 457 us -> 184 us (0.40)
  the two profiles are of different devices: /device:TPU:6 before, /device:TPU:5 now
where the time goes in v2:
time: 184 us; the launch traced here: 183 us
  Pallas kernels  179 us (97%)
  local copies, waits for them, and re-layouts  3.61 us (2%)
    pallas_call x1, Pallas kernels, on_device(): pl.pallas_call(gather, name='gather', out_shape=(tile,) * 5, in_specs=[hb...  174 us
    pallas_call x1, Pallas kernels, on_device(): pl.pallas_call(finish, name='finish', grid=(ROWS // BAND,), out_shape=(ti...  5.29 us

profile of v2, /device:TPU:5, one launch (start us, length us, event | category | flops | bytes accessed | tf_op | source)
XLA Modules:
  0.0 183.3 jit_solution(7148670072736787204)
XLA Ops:
  0.6 0.0 copy-start
  0.6 0.9 copy-done
  1.5 0.0 copy-start.1
  1.5 0.9 copy-done.1
  2.4 0.0 copy-start.2
  2.4 0.9 copy-done.2
  3.3 0.0 copy-start.3
  3.3 0.9 copy-done.3
  4.3 173.8 %gather.1 = (f32[32,128,256]{2,1,0:T(8,128)S(1)}, f32[32,128,256]{2,1,0:T(8,128)S(1)}, f32[32,128,256]{2,1,0:T(8,128)S(1)}, f32[32,128,256]{2,1,0:T(8,128)S(1)}, f32[32,128,256]{2,1,0:T(8,128)S(1)}) custom-call(f32[2,256,2048]{2,1,0:T(8,128)} %theta_in.1, f32[2,256,2048]{2,1,0:T(8,128)} %press_in.1, f32[2,256,2048]{2,1,0:T(8,128)} %wind_in.1, ...), custom_call_target="tpu_custom_call" | custom-call | tf_op jit(solution)/shard_map/gather/pallas_call | solution.py:336
  178.0 5.3 %finish.1 = (f32[32,128,256]{2,1,0:T(8,128)}, f32[32,128,256]{2,1,0:T(8,128)}) custom-call(f32[32,128,256]{2,1,0:T(8,128)S(1)} %get-tuple-element.7.forcing, f32[32,128,256]{2,1,0:T(8,128)S(1)} %get-tuple-element.8.lifted, f32[32,128,256]{2,1,0:T(8,128)S(1)} %get-tuple-element.9.couple, f32[32,128,256]{2,1,0:T(8,128)S(1)} %get-tuple-element.10.inverse, ...), custom_call_target="tpu_custom_call" | custom-call | tf_op jit(solution)/shard_map/finish/pallas_call | solution.py:362
Async XLA Ops:
  0.6 0.9 copy-start
  1.5 0.9 copy-start.1
  2.4 0.9 copy-start.2
  3.3 0.9 copy-start.3

commit v3 on v2

--- a/solution.py
+++ b/solution.py
@@ -13,7 +13,7 @@
 
 LEVELS, ROWS, COLS = 32, 128, 256
 SLAB_ROWS, SLAB_COLS = 256, 2048
-PIECE = 32
+PIECE = 16
 BAND = 16
 MIB = 1024 * 1024
 
@@ -28,33 +28,35 @@
     pltpu.make_async_copy(ref, ref, sem).wait()
 
 
-def send_pieces(srcs, dsts, sends, recvs, pair):
+def send_pieces(srcs, dsts, sends, recvs, shifts, first, last):
     gx, gy = lax.axis_index("gx"), lax.axis_index("gy")
     z, c, y = (gx // 2) % 4, gx % 2, gy % 4
-    starts = []
-    for a in range(len(srcs)):
-        for r in range(ROWS // PIECE):
+
+    def piece(r, _):
+        for a in range(len(srcs)):
             for core in range(2):
-                for shift in (pair, pair + 2):
+                for shift in shifts:
                     for half in range(2):
-                        starts.append((a, r, core, shift, half))
-    for a, r, core, shift, half in starts:
-        c_to = (c + core) % 2
-        gx_to = gy * 2 + c_to
-        gy_to = half * 4 + (y + shift - z + 4) % 4
-        rows = pl.ds(pl.multiple_of(c_to * ROWS + r * PIECE, PIECE), PIECE)
-        cols = pl.ds(pl.multiple_of(gy_to * COLS, COLS), COLS)
-
-        @pl.when(jnp.logical_not((gx_to == gx) & (gy_to == gy)))
-        def _():
-            remote(
-                srcs[a].at[:, rows, cols],
-                dsts[a].at[pl.ds(gx * 2, 2), pl.ds(r * PIECE, PIECE)],
-                sends[a],
-                recvs[a],
-                gx_to,
-                gy_to,
-            ).start()
+                        c_to = (c + core) % 2
+                        gx_to = gy * 2 + c_to
+                        gy_to = half * 4 + (y + shift - z + 4) % 4
+                        rows = pl.ds(pl.multiple_of(c_to * ROWS + r * PIECE, PIECE), PIECE)
+                        cols = pl.ds(pl.multiple_of(gy_to * COLS, COLS), COLS)
+
+                        @pl.when(jnp.logical_not((gx_to == gx) & (gy_to == gy)))
+                        def _():
+                            remote(
+                                srcs[a].at[:, rows, cols],
+                                dsts[a].at[pl.ds(gx * 2, 2), pl.ds(pl.multiple_of(r * PIECE, PIECE), PIECE)],
+                                sends[a],
+                                recvs[a],
+                                gx_to,
+                                gy_to,
+                            ).start()
+        return 0
+
+    count = ROWS // PIECE
+    lax.fori_loop(count * first // 4, count * last // 4, piece, 0)
 
 
 def smooth_wind(wind, smoothed):
@@ -208,11 +210,6 @@
         )
         for a, (src, dst) in enumerate(((theta_in, theta), (press_in, press)))
     ]
-    for pair in range(2):
-        send_pieces(
-            (theta_in, press_in), (theta, press),
-            (send.at[0], send.at[1]), (recv.at[0], recv.at[1]), pair,
-        )
     for load in loads:
         load.start()
 
@@ -221,6 +218,7 @@
         for copy in own:
             copy.start()
 
+    send_pieces((theta_in, press_in), (theta, press), (send.at[0], send.at[1]), (recv.at[0], recv.at[1]), (0, 2, 1, 3), 0, 1)
     blank = jnp.zeros((1, SLAB_COLS), jnp.float32)
 
     @pl.when(jnp.logical_not(low_y))
@@ -243,7 +241,8 @@
         for level in range(2):
             forcing[gx * 2 + level] = smoothed[level, own_rows, own_cols]
 
-    send_pieces((smoothed,), (forcing,), (send.at[2],), (recv.at[2],), 0)
+    send_pieces((theta_in, press_in), (theta, press), (send.at[0], send.at[1]), (recv.at[0], recv.at[1]), (0, 2, 1, 3), 1, 4)
+    send_pieces((smoothed,), (forcing,), (send.at[2],), (recv.at[2],), (0, 2, 1, 3), 0, 4)
 
     for load in loads[1:]:
         load.wait()
@@ -282,7 +281,6 @@
     pl.when(low_x)(lambda: geo_down.start())
     pl.when(high_y)(lambda: geo_right.start())
     pl.when(low_y)(lambda: geo_left.start())
-    send_pieces((smoothed,), (forcing,), (send.at[2],), (recv.at[2],), 1)
 
     pl.when(low_x)(lambda: geo_up.wait_recv())
     pl.when(high_x)(lambda: geo_down.wait_recv())

time: 184 us -> 167 us (0.908)
  Pallas kernels: 179 us -> 161 us
    pallas_call x1, Pallas kernels: 174 us -> 156 us  [on_device(): pl.pallas_call(gather, name='gather', out_shape=(tile,) * 5, in_specs=[hb...]
where the time goes in v3:
time: 167 us; the launch traced here: 166 us
  Pallas kernels  161 us (96%)
  local copies, waits for them, and re-layouts  3.61 us (2%)
    pallas_call x1, Pallas kernels, on_device(): pl.pallas_call(gather, name='gather', out_shape=(tile,) * 5, in_specs=[hb...  156 us
    pallas_call x1, Pallas kernels, on_device(): pl.pallas_call(finish, name='finish', grid=(ROWS // BAND,), out_shape=(ti...  5.29 us
    unnamed x8, local copies, waits for them, and re-layouts  3.61 us

profile of v3, /device:TPU:5, one launch (start us, length us, event | category | flops | bytes accessed | tf_op | source)
XLA Modules:
  0.0 165.6 jit_solution(13379208282582200290)
XLA Ops:
  0.6 0.0 copy-start
  0.6 0.9 copy-done
  1.5 0.0 copy-start.1
  1.5 0.9 copy-done.1
  2.4 0.0 copy-start.2
  2.4 0.9 copy-done.2
  3.3 0.0 copy-start.3
  3.3 0.9 copy-done.3
  4.3 156.0 %gather.1 = (f32[32,128,256]{2,1,0:T(8,128)S(1)}, f32[32,128,256]{2,1,0:T(8,128)S(1)}, f32[32,128,256]{2,1,0:T(8,128)S(1)}, f32[32,128,256]{2,1,0:T(8,128)S(1)}, f32[32,128,256]{2,1,0:T(8,128)S(1)}) custom-call(f32[2,256,2048]{2,1,0:T(8,128)} %theta_in.1, f32[2,256,2048]{2,1,0:T(8,128)} %press_in.1, f32[2,256,2048]{2,1,0:T(8,128)} %wind_in.1, ...), custom_call_target="tpu_custom_call" | custom-call | tf_op jit(solution)/shard_map/gather/pallas_call | solution.py:334
  160.3 5.3 %finish.1 = (f32[32,128,256]{2,1,0:T(8,128)}, f32[32,128,256]{2,1,0:T(8,128)}) custom-call(f32[32,128,256]{2,1,0:T(8,128)S(1)} %get-tuple-element.7.forcing, f32[32,128,256]{2,1,0:T(8,128)S(1)} %get-tuple-element.8.lifted, f32[32,128,256]{2,1,0:T(8,128)S(1)} %get-tuple-element.9.couple, f32[32,128,256]{2,1,0:T(8,128)S(1)} %get-tuple-element.10.inverse, ...), custom_call_target="tpu_custom_call" | custom-call | tf_op jit(solution)/shard_map/finish/pallas_call | solution.py:360
Async XLA Ops:
  0.6 0.9 copy-start
  1.5 0.9 copy-start.1
  2.4 0.9 copy-start.2
  3.3 0.9 copy-start.3

commit v4 on v3

v4 whole, which is shorter than its diff:
```python
import jax
import jax.numpy as jnp
from jax import lax
from jax.experimental import pallas as pl
from jax.experimental.pallas import tpu as pltpu
from jax.sharding import PartitionSpec as P

gamma_ratio = 1.4
smooth_rate = 0.2
lift_rate = 0.3
couple_rate = 0.5
land_boost = 0.5

LEVELS, ROWS, COLS = 32, 128, 256
SLAB_ROWS, SLAB_COLS = 256, 2048
PIECE = 16
BAND = 16
QUARTER = ROWS // 4
EARLY = 2
MIB = 1024 * 1024
GATHER_MIB = 44


def remote(src, dst, send, recv, gx, gy):
    return pltpu.make_async_remote_copy(
        src, dst, send, recv, device_id={"gx": gx, "gy": gy}, device_id_type=pl.DeviceIdType.MESH
    )


def await_bytes(ref, sem):
    pltpu.make_async_copy(ref, ref, sem).wait()


def send_quarter(srcs, dsts, sends, recvs, quarter):
    gx, gy = lax.axis_index("gx"), lax.axis_index("gy")
    z, c, y = (gx // 2) % 4, gx % 2, gy % 4

    def piece(r, _):
        at = pl.multiple_of(r * PIECE, PIECE)
        for a in range(len(srcs)):
            for core in range(2):
                for shift in (0, 2, 1, 3):
                    for half in range(2):
                        c_to = (c + core) % 2
                        gx_to = gy * 2 + c_to
                        gy_to = half * 4 + (y + shift - z + 4) % 4
                        rows = pl.ds(pl.multiple_of(c_to * ROWS + at, PIECE), PIECE)
                        cols = pl.ds(pl.multiple_of(gy_to * COLS, COLS), COLS)

                        @pl.when(jnp.logical_not((gx_to == gx) & (gy_to == gy)))
                        def _():
                            remote(
                                srcs[a].at[:, rows, cols],
                                dsts[a].at[pl.ds(gx * 2, 2), pl.ds(at, PIECE)],
                                sends[a],
                                recvs[a],
                                gx_to,
                                gy_to,
                            ).start()
        return 0

    count = QUARTER // PIECE
    lax.fori_loop(quarter * count, quarter * count + count, piece, 0)


def smooth_wind(wind, smoothed):
    sub = lax.broadcasted_iota(jnp.int32, (8, SLAB_COLS), 0)
    lane = lax.broadcasted_iota(jnp.int32, (8, SLAB_COLS), 1)
    for level in range(2):

        def block(b, _):
            at = pl.multiple_of(b * 8, 8)
            before = wind[level, pl.ds(at, 8), :]
            here = wind[level, pl.ds(pl.multiple_of(at + 8, 8), 8), :]
            after = wind[level, pl.ds(pl.multiple_of(at + 16, 8), 8), :]
            low = jnp.where(sub == 0, pltpu.roll(before, 1, 0), pltpu.roll(here, 1, 0))
            high = jnp.where(sub == 7, pltpu.roll(after, 7, 0), pltpu.roll(here, 7, 0))
            left = jnp.where(lane == 0, 0.0, pltpu.roll(here, 1, 1))
            right = jnp.where(lane == SLAB_COLS - 1, 0.0, pltpu.roll(here, SLAB_COLS - 1, 1))
            lap = high + low + right + left - 4.0 * here
            smoothed[level, pl.ds(at, 8), :] = here + smooth_rate * lap
            return 0

        lax.fori_loop(0, SLAB_ROWS // 8, block, 0)


def columns(theta, press, terrain, mass, land, top, geo, couple, inverse, quarter):
    def band(b, _):
        rows = pl.ds(pl.multiple_of(b * BAND, BAND), BAND)
        ground, weight = terrain[rows, :], mass[rows, :]
        limit = jnp.where(land[rows, :] > 0, top[rows, :], 0)

        def state(k, rising):
            p = press[k, rows, :]
            alpha = theta[k, rows, :] * jnp.exp(-jnp.log(p) / gamma_ratio)
            rising = rising + alpha
            geo[k, rows, :] = ground + weight * rising / LEVELS
            return rising, gamma_ratio * p * alpha

        def eliminate(k, below, above, ratio):
            damping = jnp.where(k < limit, 1.0 + land_boost, 1.0)
            denom = damping + below + above - below * ratio
            inv = 1.0 / denom
            inverse[k, rows, :] = inv
            couple[k, rows, :] = above
            return above * inv

        def level(k, carry):
            rising, sound_low, below, ratio = carry
            rising, sound = state(k, rising)
            above = couple_rate * 0.5 * (sound_low + sound)
            ratio = eliminate(k - 1, below, above, ratio)
            return rising, sound, above, ratio

        zero = jnp.zeros((BAND, COLS), jnp.float32)
        rising, sound = state(0, zero)
        _, _, below, ratio = lax.fori_loop(1, LEVELS, level, (rising, sound, zero, zero))
        eliminate(LEVELS - 1, below, zero, ratio)
        return 0

    count = QUARTER // BAND
    lax.fori_loop(quarter * count, quarter * count + count, band, 0)


def pack_columns(geo, packed, quarter):
    rows = pl.ds(quarter * QUARTER, QUARTER)
    lane = lax.broadcasted_iota(jnp.int32, (QUARTER, 128), 1)

    def level(k, carry):
        last = pltpu.roll(geo[k, rows, COLS - 128 :], k + 1, 1)
        first = pltpu.roll(geo[k, rows, :128], k, 1)
        return jnp.where(lane == k, last, carry[0]), jnp.where(lane == k, first, carry[1])

    zero = jnp.zeros((QUARTER, 128), jnp.float32)
    last, first = lax.fori_loop(0, LEVELS, level, (zero, zero))
    packed[0, rows, :] = last
    packed[1, rows, :] = first


def lift(geo, edge_rows, edge_cols, out):
    sub = lax.broadcasted_iota(jnp.int32, (ROWS, COLS), 0)
    lane = lax.broadcasted_iota(jnp.int32, (ROWS, 128), 1)

    def level(k, _):
        here = geo[k]
        low = jnp.where(sub == 0, edge_rows[0, k], pltpu.roll(here, 1, 0))
        high = jnp.where(sub == ROWS - 1, edge_rows[1, k], pltpu.roll(here, ROWS - 1, 0))
        left = pltpu.roll(here, 1, 1)
        right = pltpu.roll(here, COLS - 1, 1)
        from_left = pltpu.roll(edge_cols[0], 128 - k, 1)
        from_right = pltpu.roll(edge_cols[1], 127 - k, 1)
        for half in range(2):
            part = slice(half * 128, half * 128 + 128)
            l, r = left[:, part], right[:, part]
            if half == 0:
                l = jnp.where(lane == 0, from_left, l)
            else:
                r = jnp.where(lane == 127, from_right, r)
            lap = high[:, part] + low[:, part] + r + l - 4.0 * here[:, part]
            out[k, :, part] = lift_rate * lap
        return 0

    lax.fori_loop(0, LEVELS, level, 0)


def solve(wind, lifted, couple, inverse, quarter):
    rows = pl.ds(quarter * QUARTER, QUARTER)
    value = (wind[0, rows, :] + lifted[0, rows, :]) * inverse[0, rows, :]
    wind[0, rows, :] = value
    for k in range(1, LEVELS):
        below = couple[k - 1, rows, :]
        value = (wind[k, rows, :] + lifted[k, rows, :] + below * value) * inverse[k, rows, :]
        wind[k, rows, :] = value
    for k in range(LEVELS - 2, -1, -1):
        value = wind[k, rows, :] + couple[k, rows, :] * inverse[k, rows, :] * value
        wind[k, rows, :] = value


def gather(
    theta_in, press_in, wind_in, terrain_in, mass_in, land_in, top_in,
    forcing, geo,
    theta, press, wind, smoothed, lifted, couple, inverse, terrain, mass, land, top,
    edge_rows, edge_cols, packed, send, recv, edge_send, edge_recv, local,
):
    gx, gy = lax.axis_index("gx"), lax.axis_index("gy")
    c = gx % 2
    stays = (gx // 2) == gy
    moves = jnp.logical_not(stays)
    own_rows = pl.ds(pl.multiple_of(c * ROWS, ROWS), ROWS)
    own_cols = pl.ds(pl.multiple_of(gy * COLS, COLS), COLS)
    own_levels = pl.ds(gx * 2, 2)
    quarters = [pl.ds(q * QUARTER, QUARTER) for q in range(4)]
    low_x, high_x, low_y, high_y = gx > 0, gx < 15, gy > 0, gy < 7

    wind_up = remote(
        wind_in.at[:, pl.ds(SLAB_ROWS - 1, 1), :], wind.at[:, pl.ds(7, 1), :],
        edge_send.at[0], edge_recv.at[0], gx, (gy + 1) % 8,
    )
    wind_down = remote(
        wind_in.at[:, pl.ds(0, 1), :], wind.at[:, pl.ds(8 + SLAB_ROWS, 1), :],
        edge_send.at[1], edge_recv.at[1], gx, (gy + 7) % 8,
    )
    geo_up = remote(
        geo.at[:, pl.ds(ROWS - 1, 1), :], edge_rows.at[0],
        edge_send.at[2], edge_recv.at[2], (gx + 1) % 16, gy,
    )
    geo_down = remote(
        geo.at[:, pl.ds(0, 1), :], edge_rows.at[1],
        edge_send.at[3], edge_recv.at[3], (gx + 15) % 16, gy,
    )
    geo_right = [
        remote(
            packed.at[0, rows], edge_cols.at[0, rows],
            edge_send.at[4 + q], edge_recv.at[4 + q], gx, (gy + 1) % 8,
        )
        for q, rows in enumerate(quarters)
    ]
    geo_left = [
        remote(
            packed.at[1, rows], edge_cols.at[1, rows],
            edge_send.at[8 + q], edge_recv.at[8 + q], gx, (gy + 7) % 8,
        )
        for q, rows in enumerate(quarters)
    ]

    pl.when(high_y)(lambda: wind_up.start())
    pl.when(low_y)(lambda: wind_down.start())
    loads = [
        pltpu.make_async_copy(wind_in, wind.at[:, pl.ds(8, SLAB_ROWS), :], local.at[0]),
        pltpu.make_async_copy(terrain_in, terrain, local.at[1]),
        pltpu.make_async_copy(mass_in, mass, local.at[2]),
        pltpu.make_async_copy(land_in, land, local.at[3]),
        pltpu.make_async_copy(top_in, top, local.at[4]),
    ]
    own = [
        pltpu.make_async_copy(
            src.at[:, own_rows, own_cols], dst.at[own_levels], local.at[5 + a]
        )
        for a, (src, dst) in enumerate(((theta_in, theta), (press_in, press)))
    ]
    for load in loads:
        load.start()

    @pl.when(stays)
    def _():
        for copy in own:
            copy.start()

    def send_state(q):
        send_quarter(
            (theta_in, press_in), (theta, press),
            (send.at[0], send.at[1]), (recv.at[q], recv.at[4 + q]), q,
        )

    def send_forcing(q):
        send_quarter((smoothed,), (forcing,), (send.at[2],), (recv.at[8 + q],), q)

    def await_quarter(refs, q):
        for count, cond in ((LEVELS - 2, stays), (LEVELS, moves)):

            @pl.when(cond)
            def _():
                for a, ref in refs:
                    await_bytes(ref.at[pl.ds(0, count), quarters[q]], recv.at[4 * a + q])

    send_state(0)

    blank = jnp.zeros((1, SLAB_COLS), jnp.float32)

    @pl.when(jnp.logical_not(low_y))
    def _():
        for level in range(2):
            wind[level, pl.ds(7, 1), :] = blank
        edge_cols[0] = jnp.zeros((ROWS, 128), jnp.float32)

    @pl.when(jnp.logical_not(high_y))
    def _():
        for level in range(2):
            wind[level, pl.ds(8 + SLAB_ROWS, 1), :] = blank
        edge_cols[1] = jnp.zeros((ROWS, 128), jnp.float32)

    @pl.when(jnp.logical_not(low_x))
    def _():
        edge_rows[0] = jnp.zeros((LEVELS, 1, COLS), jnp.float32)

    @pl.when(jnp.logical_not(high_x))
    def _():
        edge_rows[1] = jnp.zeros((LEVELS, 1, COLS), jnp.float32)

    loads[0].wait()
    pl.when(low_y)(lambda: wind_up.wait_recv())
    pl.when(high_y)(lambda: wind_down.wait_recv())
    smooth_wind(wind, smoothed)

    @pl.when(stays)
    def _():
        for level in range(2):
            forcing[gx * 2 + level] = smoothed[level, own_rows, own_cols]

    for q in range(1, 4):
        send_state(q)
    for q in range(EARLY):
        send_forcing(q)

    for load in loads[1:]:
        load.wait()

    @pl.when(stays)
    def _():
        for copy in own:
            copy.wait()

    for q in range(4):
        await_quarter(((0, theta), (1, press)), q)
        columns(theta, press, terrain, mass, land, top, geo, couple, inverse, q)
        pack_columns(geo, packed, q)
        if q == 0:
            pl.when(low_x)(lambda: geo_down.start())
        if q == 3:
            pl.when(high_x)(lambda: geo_up.start())
        pl.when(high_y)(lambda: geo_right[q].start())
        pl.when(low_y)(lambda: geo_left[q].start())

    for q in range(EARLY, 4):
        send_forcing(q)

    pl.when(low_x)(lambda: geo_up.wait_recv())
    pl.when(high_x)(lambda: geo_down.wait_recv())

    @pl.when(low_y)
    def _():
        for copy in geo_right:
            copy.wait_recv()

    @pl.when(high_y)
    def _():
        for copy in geo_left:
            copy.wait_recv()

    lift(geo, edge_rows, edge_cols, lifted)
    for q in range(4):
        await_quarter(((2, forcing),), q)
        solve(forcing, lifted, couple, inverse, q)

    for cond, copies in (
        (high_x, (geo_up,)),
        (low_x, (geo_down,)),
        (high_y, (wind_up, *geo_right)),
        (low_y, (wind_down, *geo_left)),
    ):

        @pl.when(cond)
        def _():
            for copy in copies:
                copy.wait_send()

    for count, cond in ((LEVELS - 2, stays), (LEVELS, moves)):

        @pl.when(cond)
        def _():
            for a, ref in enumerate((theta, press, forcing)):
                await_bytes(ref.at[pl.ds(0, count)], send.at[a])


def store(wind, geo, wind_out, geo_out, sems):
    copies = []
    for n, (src, dst) in enumerate(((wind, wind_out), (geo, geo_out))):
        for part in range(4):
            levels = pl.ds(part * 8, 8)
            copies.append(pltpu.make_async_copy(src.at[levels], dst.at[levels], sems.at[n, part]))
    for copy in copies:
        copy.start()
    for copy in copies:
        copy.wait()


def on_device(*args):
    tile = jax.ShapeDtypeStruct((LEVELS, ROWS, COLS), jnp.float32)
    hbm = pl.BlockSpec(memory_space=pltpu.HBM)
    vmem = pl.BlockSpec(memory_space=pltpu.VMEM)
    f32, i32 = jnp.float32, jnp.int32
    parts = pl.pallas_call(
        gather,
        name="gather",
        out_shape=(tile,) * 2,
        in_specs=[hbm] * 7,
        out_specs=(vmem,) * 2,
        scratch_shapes=[
            pltpu.VMEM((LEVELS, ROWS, COLS), f32),
            pltpu.VMEM((LEVELS, ROWS, COLS), f32),
            pltpu.VMEM((2, SLAB_ROWS + 16, SLAB_COLS), f32),
            pltpu.VMEM((2, SLAB_ROWS, SLAB_COLS), f32),
            pltpu.VMEM((LEVELS, ROWS, COLS), f32),
            pltpu.VMEM((LEVELS, ROWS, COLS), f32),
            pltpu.VMEM((LEVELS, ROWS, COLS), f32),
            pltpu.VMEM((ROWS, COLS), f32),
            pltpu.VMEM((ROWS, COLS), f32),
            pltpu.VMEM((ROWS, COLS), i32),
            pltpu.VMEM((ROWS, COLS), i32),
            pltpu.VMEM((2, LEVELS, 1, COLS), f32),
            pltpu.VMEM((2, ROWS, 128), f32),
            pltpu.VMEM((2, ROWS, 128), f32),
            pltpu.SemaphoreType.DMA((3,)),
            pltpu.SemaphoreType.DMA((12,)),
            pltpu.SemaphoreType.DMA((12,)),
            pltpu.SemaphoreType.DMA((12,)),
            pltpu.SemaphoreType.DMA((7,)),
        ],
        compiler_params=pltpu.CompilerParams(
            has_side_effects=True, vmem_limit_bytes=GATHER_MIB * MIB
        ),
    )(*(pltpu.with_memory_space_constraint(x, pltpu.HBM) for x in args))
    return pl.pallas_call(
        store,
        name="store",
        out_shape=(tile, tile),
        in_specs=[vmem] * 2,
        out_specs=(hbm, hbm),
        scratch_shapes=[pltpu.SemaphoreType.DMA((2, 4))],
        compiler_params=pltpu.CompilerParams(vmem_limit_bytes=1 * MIB),
    )(*parts)


def solution(mesh):
    slab, tile = P("gx", "gy", None), P("gx", "gy")
    return jax.shard_map(
        on_device,
        mesh=mesh,
        in_specs=(slab,) * 3 + (tile,) * 4,
        out_specs=(P(None, "gx", "gy"),) * 2,
        check_vma=False,
    )
```

time: 167 us -> 211 us (1.26)
  Pallas kernels: 161 us -> 208 us
  local copies, waits for them, and re-layouts: 3.61 us -> 0 us
    pallas_call x2, Pallas kernels: 161 us -> 208 us  [the longest x1 204 us: on_device(): pl.pallas_call(gather, name='gather', out_shape=(tile,) * 2, in_specs=[hb...]
    unnamed x8 -> x0, local copies, waits for them, and re-layouts: 3.61 us -> none
where the time goes in v4:
time: 211 us; the launch traced here: 208 us
  Pallas kernels  208 us (99%)
    pallas_call x1, Pallas kernels, on_device(): pl.pallas_call(gather, name='gather', out_shape=(tile,) * 2, in_specs=[hb...  204 us

profile of v4, /device:TPU:5, one launch (start us, length us, event | category | flops | bytes accessed | tf_op | source)
XLA Modules:
  0.0 208.2 jit_solution(9975948931213417615)
XLA Ops:
  0.6 204.2 %gather.1 = (f32[32,128,256]{2,1,0:T(8,128)S(1)}, f32[32,128,256]{2,1,0:T(8,128)S(1)}) custom-call(f32[2,256,2048]{2,1,0:T(8,128)} %theta_in.1, f32[2,256,2048]{2,1,0:T(8,128)} %press_in.1, f32[2,256,2048]{2,1,0:T(8,128)} %wind_in.1, f32[128,256]{1,0:T(8,128)} %terrain_in.1, f32[128,256]{1,0:T(8,128)} %mass_in.1, s32[128,256]{1,0:T(8,128)} %land_in.1, ...), custom_call_target="tpu_custom_call" | custom-call | tf_op jit(solution)/shard_map/gather/pallas_call | solution.py:382
  204.9 3.4 %store.1 = (f32[32,128,256]{2,1,0:T(8,128)}, f32[32,128,256]{2,1,0:T(8,128)}) custom-call(f32[32,128,256]{2,1,0:T(8,128)S(1)} %get-tuple-element.4.wind, f32[32,128,256]{2,1,0:T(8,128)S(1)} %get-tuple-element.5.geo), custom_call_target="tpu_custom_call" | custom-call | tf_op jit(solution)/shard_map/store/pallas_call | solution.py:413

commit v5 on v4

--- a/solution.py
+++ b/solution.py
@@ -125,16 +125,18 @@
 def pack_columns(geo, packed, quarter):
     rows = pl.ds(quarter * QUARTER, QUARTER)
     lane = lax.broadcasted_iota(jnp.int32, (QUARTER, 128), 1)
+    base = quarter * LEVELS
 
     def level(k, carry):
-        last = pltpu.roll(geo[k, rows, COLS - 128 :], k + 1, 1)
-        first = pltpu.roll(geo[k, rows, :128], k, 1)
-        return jnp.where(lane == k, last, carry[0]), jnp.where(lane == k, first, carry[1])
-
-    zero = jnp.zeros((QUARTER, 128), jnp.float32)
-    last, first = lax.fori_loop(0, LEVELS, level, (zero, zero))
-    packed[0, rows, :] = last
-    packed[1, rows, :] = first
+        at = base + k
+        last = pltpu.roll(geo[k, rows, COLS - 128 :], (at + 1) % 128, 1)
+        first = pltpu.roll(geo[k, rows, :128], at, 1)
+        return jnp.where(lane == at, last, carry[0]), jnp.where(lane == at, first, carry[1])
+
+    carry = (jnp.zeros((QUARTER, 128), jnp.float32),) * 2 if quarter == 0 else (packed[0], packed[1])
+    last, first = lax.fori_loop(0, LEVELS, level, carry)
+    packed[0] = last
+    packed[1] = first
 
 
 def lift(geo, edge_rows, edge_cols, out):
@@ -147,8 +149,13 @@
         high = jnp.where(sub == ROWS - 1, edge_rows[1, k], pltpu.roll(here, ROWS - 1, 0))
         left = pltpu.roll(here, 1, 1)
         right = pltpu.roll(here, COLS - 1, 1)
-        from_left = pltpu.roll(edge_cols[0], 128 - k, 1)
-        from_right = pltpu.roll(edge_cols[1], 127 - k, 1)
+        west, east = edge_cols[0], edge_cols[1]
+        from_left = jnp.concatenate(
+            [pltpu.roll(west, (128 - LEVELS * q - k) % 128, 1) for q in range(4)], 0
+        )
+        from_right = jnp.concatenate(
+            [pltpu.roll(east, 127 - LEVELS * q - k, 1) for q in range(4)], 0
+        )
         for half in range(2):
             part = slice(half * 128, half * 128 + 128)
             l, r = left[:, part], right[:, part]
@@ -208,20 +215,12 @@
         geo.at[:, pl.ds(0, 1), :], edge_rows.at[1],
         edge_send.at[3], edge_recv.at[3], (gx + 15) % 16, gy,
     )
-    geo_right = [
-        remote(
-            packed.at[0, rows], edge_cols.at[0, rows],
-            edge_send.at[4 + q], edge_recv.at[4 + q], gx, (gy + 1) % 8,
-        )
-        for q, rows in enumerate(quarters)
-    ]
-    geo_left = [
-        remote(
-            packed.at[1, rows], edge_cols.at[1, rows],
-            edge_send.at[8 + q], edge_recv.at[8 + q], gx, (gy + 7) % 8,
-        )
-        for q, rows in enumerate(quarters)
-    ]
+    geo_right = remote(
+        packed.at[0], edge_cols.at[0], edge_send.at[4], edge_recv.at[4], gx, (gy + 1) % 8
+    )
+    geo_left = remote(
+        packed.at[1], edge_cols.at[1], edge_send.at[5], edge_recv.at[5], gx, (gy + 7) % 8
+    )
 
     pl.when(high_y)(lambda: wind_up.start())
     pl.when(low_y)(lambda: wind_down.start())
@@ -240,6 +239,8 @@
     ]
     for load in loads:
         load.start()
+    for load in loads:
+        load.wait()
 
     @pl.when(stays)
     def _():
@@ -271,13 +272,13 @@
     def _():
         for level in range(2):
             wind[level, pl.ds(7, 1), :] = blank
-        edge_cols[0] = jnp.zeros((ROWS, 128), jnp.float32)
+        edge_cols[0] = jnp.zeros((QUARTER, 128), jnp.float32)
 
     @pl.when(jnp.logical_not(high_y))
     def _():
         for level in range(2):
             wind[level, pl.ds(8 + SLAB_ROWS, 1), :] = blank
-        edge_cols[1] = jnp.zeros((ROWS, 128), jnp.float32)
+        edge_cols[1] = jnp.zeros((QUARTER, 128), jnp.float32)
 
     @pl.when(jnp.logical_not(low_x))
     def _():
@@ -287,7 +288,6 @@
     def _():
         edge_rows[1] = jnp.zeros((LEVELS, 1, COLS), jnp.float32)
 
-    loads[0].wait()
     pl.when(low_y)(lambda: wind_up.wait_recv())
     pl.when(high_y)(lambda: wind_down.wait_recv())
     smooth_wind(wind, smoothed)
@@ -302,8 +302,6 @@
     for q in range(EARLY):
         send_forcing(q)
 
-    for load in loads[1:]:
-        load.wait()
 
     @pl.when(stays)
     def _():
@@ -316,10 +314,9 @@
         pack_columns(geo, packed, q)
         if q == 0:
             pl.when(low_x)(lambda: geo_down.start())
-        if q == 3:
-            pl.when(high_x)(lambda: geo_up.start())
-        pl.when(high_y)(lambda: geo_right[q].start())
-        pl.when(low_y)(lambda: geo_left[q].start())
+    pl.when(high_x)(lambda: geo_up.start())
+    pl.when(high_y)(lambda: geo_right.start())
+    pl.when(low_y)(lambda: geo_left.start())
 
     for q in range(EARLY, 4):
         send_forcing(q)
@@ -327,16 +324,8 @@
     pl.when(low_x)(lambda: geo_up.wait_recv())
     pl.when(high_x)(lambda: geo_down.wait_recv())
 
-    @pl.when(low_y)
-    def _():
-        for copy in geo_right:
-            copy.wait_recv()
-
-    @pl.when(high_y)
-    def _():
-        for copy in geo_left:
-            copy.wait_recv()
-
+    pl.when(low_y)(lambda: geo_right.wait_recv())
+    pl.when(high_y)(lambda: geo_left.wait_recv())
     lift(geo, edge_rows, edge_cols, lifted)
     for q in range(4):
         await_quarter(((2, forcing),), q)
@@ -345,8 +334,8 @@
     for cond, copies in (
         (high_x, (geo_up,)),
         (low_x, (geo_down,)),
-        (high_y, (wind_up, *geo_right)),
-        (low_y, (wind_down, *geo_left)),
+        (high_y, (wind_up, geo_right)),
+        (low_y, (wind_down, geo_left)),
     ):
 
         @pl.when(cond)
@@ -398,12 +387,12 @@
             pltpu.VMEM((ROWS, COLS), i32),
             pltpu.VMEM((ROWS, COLS), i32),
             pltpu.VMEM((2, LEVELS, 1, COLS), f32),
-            pltpu.VMEM((2, ROWS, 128), f32),
-            pltpu.VMEM((2, ROWS, 128), f32),
+            pltpu.VMEM((2, QUARTER, 128), f32),
+            pltpu.VMEM((2, QUARTER, 128), f32),
             pltpu.SemaphoreType.DMA((3,)),
             pltpu.SemaphoreType.DMA((12,)),
-            pltpu.SemaphoreType.DMA((12,)),
-            pltpu.SemaphoreType.DMA((12,)),
+            pltpu.SemaphoreType.DMA((6,)),
+            pltpu.SemaphoreType.DMA((6,)),
             pltpu.SemaphoreType.DMA((7,)),
         ],
         compiler_params=pltpu.CompilerParams(

time: 211 us -> 163 us (0.77); the launches traced: 208 us -> 163 us
  Pallas kernels: 208 us -> 162 us
    pallas_call x1, Pallas kernels: 204 us -> 159 us  [on_device(): pl.pallas_call(gather, name='gather', out_shape=(tile,) * 2, in_specs=[hb...]
where the time goes in v5:
time: 163 us
  Pallas kernels  162 us (99%)
    pallas_call x1, Pallas kernels, on_device(): pl.pallas_call(gather, name='gather', out_shape=(tile,) * 2, in_specs=[hb...  159 us
    pallas_call x1, Pallas kernels, on_device(): pl.pallas_call(store, name='store', out_shape=(tile, tile), in_specs=[vme...  3.37 us

profile of v5, /device:TPU:5, one launch (start us, length us, event | category | flops | bytes accessed | tf_op | source)
XLA Modules:
  0.0 163.0 jit_solution(13069344865220512446)
XLA Ops:
  0.6 159.0 %gather.1 = (f32[32,128,256]{2,1,0:T(8,128)S(1)}, f32[32,128,256]{2,1,0:T(8,128)S(1)}) custom-call(f32[2,256,2048]{2,1,0:T(8,128)} %theta_in.1, f32[2,256,2048]{2,1,0:T(8,128)} %press_in.1, f32[2,256,2048]{2,1,0:T(8,128)} %wind_in.1, f32[128,256]{1,0:T(8,128)} %terrain_in.1, f32[128,256]{1,0:T(8,128)} %mass_in.1, s32[128,256]{1,0:T(8,128)} %land_in.1, ...), custom_call_target="tpu_custom_call" | custom-call | tf_op jit(solution)/shard_map/gather/pallas_call | solution.py:371
  159.6 3.4 %store.1 = (f32[32,128,256]{2,1,0:T(8,128)}, f32[32,128,256]{2,1,0:T(8,128)}) custom-call(f32[32,128,256]{2,1,0:T(8,128)S(1)} %get-tuple-element.4.wind, f32[32,128,256]{2,1,0:T(8,128)S(1)} %get-tuple-element.5.geo), custom_call_target="tpu_custom_call" | custom-call | tf_op jit(solution)/shard_map/store/pallas_call | solution.py:402

commit v6 on v5

--- a/solution.py
+++ b/solution.py
@@ -13,7 +13,7 @@
 
 LEVELS, ROWS, COLS = 32, 128, 256
 SLAB_ROWS, SLAB_COLS = 256, 2048
-PIECE = 16
+PIECE = 8
 BAND = 16
 QUARTER = ROWS // 4
 EARLY = 2

time: 163 us -> 163 us (level)
  no operation moved by 1% of the time
where the time goes in v6:
time: 163 us
  Pallas kernels  162 us (99%)
    pallas_call x1, Pallas kernels, on_device(): pl.pallas_call(gather, name='gather', out_shape=(tile,) * 2, in_specs=[hb...  159 us
    pallas_call x1, Pallas kernels, on_device(): pl.pallas_call(store, name='store', out_shape=(tile, tile), in_specs=[vme...  3.37 us

profile of v6, /device:TPU:5, one launch (start us, length us, event | category | flops | bytes accessed | tf_op | source)
XLA Modules:
  0.0 162.6 jit_solution(10744796839860603561)
XLA Ops:
  0.6 158.6 %gather.1 = (f32[32,128,256]{2,1,0:T(8,128)S(1)}, f32[32,128,256]{2,1,0:T(8,128)S(1)}) custom-call(f32[2,256,2048]{2,1,0:T(8,128)} %theta_in.1, f32[2,256,2048]{2,1,0:T(8,128)} %press_in.1, f32[2,256,2048]{2,1,0:T(8,128)} %wind_in.1, f32[128,256]{1,0:T(8,128)} %terrain_in.1, f32[128,256]{1,0:T(8,128)} %mass_in.1, s32[128,256]{1,0:T(8,128)} %land_in.1, ...), custom_call_target="tpu_custom_call" | custom-call | tf_op jit(solution)/shard_map/gather/pallas_call | solution.py:371
  159.2 3.4 %store.1 = (f32[32,128,256]{2,1,0:T(8,128)}, f32[32,128,256]{2,1,0:T(8,128)}) custom-call(f32[32,128,256]{2,1,0:T(8,128)S(1)} %get-tuple-element.4.wind, f32[32,128,256]{2,1,0:T(8,128)S(1)} %get-tuple-element.5.geo), custom_call_target="tpu_custom_call" | custom-call | tf_op jit(solution)/shard_map/store/pallas_call | solution.py:402
